TPU v7x, 128 devices: a whole 4x4x4 slice. The times are simulated.
128 devices in a mesh: rows: 16 (over y_hi, z, core), tiles: 8 (over y_lo, x).
Axes of the slice: x: 4, y: 4 (y_hi: 2, y_lo: 2; y = y_hi * 2 + y_lo), z: 4, core: 2. Of those that a mesh axis runs over, the one named last changes fastest.
Arguments:
- features: bfloat16 [16384, 16384], P(('rows', 'tiles')), as said below
- row_salt: int32 [16384], P(('rows', 'tiles')), may hold values from 0 to 32767
- column_multiplier: int32 [16384], replicated, may hold values from 1 to 32767
- column_offset: int32 [16384], replicated, may hold values from 0 to 65520
- thresholds: int32 [16384], replicated, may hold values from 16000 to 65520
Outputs:
- similarity: float32 [256, 16384], P('rows', 'tiles')
Inputs may be any that keep to these rules, and one draw needn't show every extreme that they name: `features`: Real-valued entries of order one.
All inputs are finite; a program needn't handle non-finite values.
Results may differ from a plain program's by a relative error of at most 0.0028.
Values sent between devices are 32-bit elements; how exact they have to be, the bound alone decides.
No kernel may reach another device: no remote copies, remote signals or barrier semaphores. Data moves between devices by JAX's collectives and lax.ppermute only.
A program may use at most 64 MiB of HBM per device.

v0:
```python
import functools

import jax
import jax.numpy as jnp
from jax import lax
from jax.experimental import pallas as pl
from jax.experimental.pallas import tpu as pltpu
from jax.sharding import PartitionSpec as P

AXES = ("rows", "tiles")
PRIME = 65521
SLOT_TILES = ((0, 1, 2), (3, 4, 5), (6, 7))
SLOT_ROWS = (96, 96, 80)


def place(index):
    rows, tiles = divmod(index, 8)
    return [tiles & 3, (rows >> 3) * 2 + (tiles >> 2), (rows >> 1) & 3], rows & 1


def index_of(chip, core):
    x, y, z = chip
    return (((y >> 1) << 3) | (z << 1) | core) * 8 + ((y & 1) << 2 | x)


def gray(v):
    return v ^ (v >> 1)


def flip(index, first, last):
    chip, core = place(index)
    for axis in range(3):
        kind = core if axis == 0 else 1 - core
        mask = first[axis] << kind | last[axis] << (1 - kind)
        chip[axis] = gray(gray(chip[axis]) ^ mask)
    return index_of(chip, core)


def moves(first, last):
    return [(i, flip(i, first, last)) for i in range(128)]


def axis_bits(axis):
    return [int(a == axis % 3) for a in range(3)]


def my_place():
    rows = lax.axis_index("rows")
    tile = lax.axis_index("tiles")
    return rows & 1, rows >> 1, tile


def tile_at(core, tile, c, xa, xb):
    high = jnp.where(core == 0, xb, xa)
    return tile ^ (c * 4 + high * 2 + (xa ^ xb))


def weight_of(threshold):
    return lax.rsqrt(threshold.astype(jnp.float32) / 65521.0)


def fold(v):
    return v - (v >> 16) * PRIME


def sample(values, salt, multiplier, offset, threshold, weight):
    residue = fold(fold(salt * multiplier + offset))
    keep = (residue < threshold) | (residue >= PRIME)
    return jnp.where(keep, values * weight, 0.0).astype(jnp.bfloat16)


def call(kernel, out_shape, in_spaces, scratch=(), limit=16, flops=1_000_000, nbytes=1 << 20):
    spaces = {"v": pltpu.VMEM, "h": pltpu.HBM}
    return pl.pallas_call(
        kernel,
        out_shape=[jax.ShapeDtypeStruct(s, d) for s, d in out_shape],
        in_specs=[pl.BlockSpec(memory_space=spaces[s]) for s in in_spaces],
        out_specs=[pl.BlockSpec(memory_space=pltpu.VMEM)] * len(out_shape),
        scratch_shapes=list(scratch),
        compiler_params=pltpu.CompilerParams(vmem_limit_bytes=limit << 20),
        cost_estimate=pl.CostEstimate(flops=flops, bytes_accessed=nbytes, transcendentals=0),
    )


ORDER = [(xa, c, xb) for xb in (0, 1) for xa in (1, 0) for c in (0, 1)]


def cast_kernel(feat, outq, out0s, outa, out0k, outb, mine, queries, block, sems):
    core, _, tile = my_place()
    copies = [pltpu.make_async_copy(feat.at[:, 0:256], queries, sems.at[16])]
    for to, half, first in ((block, 1 - core, 0), (mine, core, 8)):
        for i, (xa, c, xb) in enumerate(ORDER):
            start = pl.multiple_of(tile_at(half, tile, c, xa, xb) * 2048 + half * 1024, 1024)
            copies.append(
                pltpu.make_async_copy(feat.at[:, pl.ds(start, 1024)], to.at[i], sems.at[first + i])
            )
    for copy in copies:
        copy.start()
    copies[0].wait()
    outq[...] = queries[...].astype(jnp.float32)
    for i in range(8):
        copies[1 + i].wait()
        if i < 4:
            out0 = out0s if i < 2 else out0k
            out0[i % 2] = block[i, :, 0:384].astype(jnp.float32)
            outa[i] = block[i, :, 384:1024].astype(jnp.float32)
        else:
            outb[i - 4] = block[i].astype(jnp.float32)
    for i in range(8):
        copies[9 + i].wait()


def cast_call(features):
    f32 = jnp.float32
    return call(
        cast_kernel,
        [
            ((128, 256), f32),
            ((2, 128, 384), f32),
            ((4, 128, 640), f32),
            ((2, 128, 384), f32),
            ((4, 128, 1024), f32),
            ((8, 128, 1024), jnp.bfloat16),
            ((128, 256), jnp.bfloat16),
        ],
        "h",
        scratch=[
            pltpu.VMEM((8, 128, 1024), jnp.bfloat16),
            pltpu.SemaphoreType.DMA((17,)),
        ],
        limit=45,
        nbytes=6 << 20,
    )(features)


def column_of(row):
    return jnp.transpose(jnp.broadcast_to(row, (128, 128)))


def column_base(core, tile, i):
    xa, c, xb = ORDER[i]
    return tile_at(core, tile, c, xa, xb) * 16 + core * 8


def sum_squares(x):
    return jnp.sum(x * x, axis=0, keepdims=True)


def own_kernel(mine, salt, mult, offs, thr, out0s, out12):
    core, _, tile = my_place()
    salts = column_of(salt[...])
    for i in range(4):
        base = column_base(core, tile, i)
        for l in range(0 if i < 2 else 3, 8):
            m, o, t = (ref[pl.ds(base + l, 1), :] for ref in (mult, offs, thr))
            x = mine[i, :, l * 128 : (l + 1) * 128].astype(jnp.float32)
            value = sample(x, salts, m, o, t, weight_of(t))
            if l < 3:
                out0s[i, :, l * 128 : (l + 1) * 128] = value
            else:
                out12[i, :, (l - 3) * 128 : (l - 2) * 128] = value


def own_call(mine, salt, mult, offs, thr):
    return call(
        own_kernel,
        [((2, 128, 384), jnp.bfloat16), ((4, 128, 640), jnp.bfloat16)],
        "vvvvv",
        limit=8,
        flops=12_000_000,
        nbytes=3 << 20,
    )(mine, salt, mult, offs, thr)


def query_kernel(
    queries, other, salt, other_salt, mult, offs, thr, q_out, salt_out, sq_out, q_all
):
    core, pair, _ = my_place()
    salts = (column_of(salt[...]), column_of(other_salt[...]))
    salt_out[0:128, :] = salts[0]
    salt_out[128:256, :] = salts[1]
    sq_out[...] = jnp.zeros_like(sq_out)
    for l in range(2):
        lanes = slice(l * 128, (l + 1) * 128)
        m, o, t = (ref[l : l + 1, :] for ref in (mult, offs, thr))
        w = weight_of(t)
        total = None
        for u in range(2):
            source = queries if u == 0 else other
            x = source[:, lanes].astype(jnp.float32)
            part = sum_squares(x)
            total = part if total is None else total + part
            value = sample(x, salts[u], m, o, t, w).astype(jnp.float32)
            q_all[lanes, u * 128 : (u + 1) * 128] = jnp.transpose(value).astype(jnp.bfloat16)
        sq_out[l : l + 1, :] = total
    for c in range(2):
        for group in range(8):
            ya, za, zb = group >> 2, group >> 1 & 1, group & 1
            z_high = jnp.where(core == 1, zb, za)
            y_high = jnp.where(core == 1, c ^ ya, ya)
            at = pair ^ (y_high * 4 + z_high * 2 + (za ^ zb))
            start = pl.multiple_of(at * 32, 32)
            q_out[c, group * 32 : (group + 1) * 32, :] = q_all[pl.ds(start, 32), :]


def query_call(queries, other, salt, other_salt, mult, offs, thr):
    return call(
        query_kernel,
        [
            ((2, 256, 256), jnp.bfloat16),
            ((256, 128), jnp.int32),
            ((8, 128), jnp.float32),
        ],
        "vvvvvvv",
        scratch=[pltpu.VMEM((256, 256), jnp.bfloat16)],
        limit=8,
        flops=4_000_000,
    )(queries, other, salt, other_salt, mult, offs, thr)


def fill(slot, places, ready, owned, others, q, salt, params, cols, blocks, extra=None):
    core, _, tile = my_place()
    lanes_of = SLOT_TILES[slot]
    n = len(lanes_of)
    for j, i in enumerate(places):
        base = column_base(core, tile, i)
        for k, l in enumerate(lanes_of):
            lanes = slice(k * 128, (k + 1) * 128)
            m, o, t = (ref[pl.ds(base + l, 1), :] for ref in params)
            w = weight_of(t)
            own = owned(j, l)
            if not ready:
                own = sample(own.astype(jnp.float32), salt[0:128, :], m, o, t, w)
            cols[j, 0:128, lanes] = own
            cols[j, 128:256, lanes] = sample(others(j, l), salt[128:256, :], m, o, t, w)
        xa, c, _ = ORDER[i]
        gram = jnp.dot(q[c], cols[j], preferred_element_type=jnp.float32)
        for group in range(8):
            ya, za, zb = group >> 2, group >> 1 & 1, group & 1
            near = (xa, ya, za)
            at = near[(slot + 1) % 3] * 8 + near[(slot + 2) % 3] * 4 + zb * 2 + (c ^ ya)
            ref = blocks[0] if near[slot] else blocks[-1]
            for k in range(n):
                ref[at, k * 32 : (k + 1) * 32, :] = gram[
                    group * 32 : (group + 1) * 32, k * 128 : (k + 1) * 128
                ]
            if extra is not None:
                ref[at, 64:72, :] = extra[0][j]
                ref[at, 72:80, :] = extra[1][...]


def tile_of(ref, j, l):
    return ref[j, :, l * 128 : (l + 1) * 128]


def gram0s_first(own, other, q, salt, mult, offs, thr, send, cols):
    owned, others = functools.partial(tile_of, own), functools.partial(tile_of, other)
    fill(0, (0, 1), True, owned, others, q, salt, (mult, offs, thr), cols, (send,))


def gram0s_second(mine, other, q, salt, mult, offs, thr, send, cols):
    fill(
        0, (4, 5), False, lambda j, l: tile_of(mine, 4 + j, l), functools.partial(tile_of, other),
        q, salt, (mult, offs, thr), cols, (send,),
    )


def gram1_first(own, other, q, salt, mult, offs, thr, send, keep, cols):
    fill(
        1, (0, 1, 2, 3), True, lambda j, l: tile_of(own, j, l - 3),
        lambda j, l: tile_of(other, j, l - 3), q, salt, (mult, offs, thr), cols, (send, keep),
    )


def gram1_second(mine, other, q, salt, mult, offs, thr, send, keep, cols):
    fill(
        1, (4, 5, 6, 7), False, lambda j, l: tile_of(mine, 4 + j, l),
        functools.partial(tile_of, other), q, salt, (mult, offs, thr), cols, (send, keep),
    )


def sum_columns(first, others, mine, extra):
    for j in range(4):
        for l in range(8):
            own = tile_of(mine, first + j, l).astype(jnp.float32)
            extra[j, l : l + 1, :] = sum_squares(own) + sum_squares(others(j, l))


def gram2_first(
    own, other, q, salt, mult, offs, thr, mine, other0s, other0k, sq_query, send, keep, cols, extra
):
    def others(j, l):
        if l >= 3:
            return tile_of(other, j, l - 3)
        return tile_of(other0s, j, l) if j < 2 else tile_of(other0k, j - 2, l)

    sum_columns(0, others, mine, extra)
    fill(
        2, (0, 1, 2, 3), True, lambda j, l: tile_of(own, j, l - 3), others,
        q, salt, (mult, offs, thr), cols, (send, keep), (extra, sq_query),
    )


def gram2_second(mine, other, q, salt, mult, offs, thr, sq_query, send, keep, cols, extra):
    others = functools.partial(tile_of, other)
    sum_columns(4, others, mine, extra)
    fill(
        2, (4, 5, 6, 7), False, lambda j, l: tile_of(mine, 4 + j, l), others,
        q, salt, (mult, offs, thr), cols, (send, keep), (extra, sq_query),
    )


def gram0k_first(mine, other, q, salt, mult, offs, thr, keep, cols):
    fill(
        0, (2, 3), False, lambda j, l: tile_of(mine, 2 + j, l), functools.partial(tile_of, other),
        q, salt, (mult, offs, thr), cols, (keep,),
    )


def gram0k_second(mine, other, q, salt, mult, offs, thr, keep, cols):
    fill(
        0, (6, 7), False, lambda j, l: tile_of(mine, 6 + j, l),
        lambda j, l: tile_of(other, 2 + j, l), q, salt, (mult, offs, thr), cols, (keep,),
    )


def gram_call(slot, kernel, outs, count, operands):
    n = len(SLOT_TILES[slot])
    scratch = [pltpu.VMEM((count, 256, n * 128), jnp.bfloat16)]
    if slot == 2:
        scratch.append(pltpu.VMEM((4, 8, 128), jnp.float32))
    return call(
        kernel,
        [((16, SLOT_ROWS[slot], 128), jnp.float32)] * outs,
        "v" * len(operands),
        scratch=scratch,
        flops=n * count * 16_000_000,
        nbytes=3 << 20,
    )(*operands)


def join_kernel(*refs):
    outs = refs[6:]
    for at in range(4):
        row = 0
        for slot in range(3):
            height = SLOT_ROWS[slot]
            outs[at][row : row + height, :] = refs[slot][at] + refs[3 + slot][at]
            row += height


def join_call(keeps, gots):
    return call(
        join_kernel, [((sum(SLOT_ROWS), 128), jnp.float32)] * 4, "v" * 6, limit=8, nbytes=2 << 20
    )(*keeps, *gots)


def last_sum_kernel(*refs):
    send, keep = refs[8:]
    core, _, _ = my_place()

    def total(start, height):
        parts = [ref[start : start + height, :] for ref in refs[:8]]
        return ((parts[0] + parts[1]) + (parts[2] + parts[3])) + (
            (parts[4] + parts[5]) + (parts[6] + parts[7])
        )

    for l in range(8):
        start = l * 32
        even, odd = total(start, 16), total(start + 16, 16)
        keep[l * 16 : (l + 1) * 16, :] = jnp.where(core == 0, even, odd)
        send[l * 16 : (l + 1) * 16, :] = jnp.where(core == 0, odd, even)
    squares = total(256, 8)
    send[128:136, :] = squares
    keep[128:136, :] = squares
    keep[136:144, :] = total(264, 8)


def last_sum_call(parts):
    return call(
        last_sum_kernel, [((136, 128), jnp.float32), ((144, 128), jnp.float32)], "v" * 8, limit=4
    )(*parts)


def finish_kernel(keep, other, out):
    core, pair, _ = my_place()
    row = pair * 2 + core
    line = jnp.broadcast_to(keep[pl.ds(136 + row // 8, 1), :], (16, 128))
    lane = lax.broadcasted_iota(jnp.int32, (16, 128), 1)
    spot = lax.broadcasted_iota(jnp.int32, (16, 128), 0) + (row % 8) * 16
    squares = jnp.sum(jnp.where(lane == spot, line, 0.0), axis=1, keepdims=True)
    query_norm = jnp.sqrt(squares + 1e-06)
    for source, half in ((keep, core), (other, 1 - core)):
        for l in range(8):
            norm = jnp.sqrt(source[128 + l : 129 + l, :] + 1e-06)
            at = pl.multiple_of(half * 1024 + l * 128, 128)
            out[:, pl.ds(at, 128)] = source[l * 16 : (l + 1) * 16, :] / (query_norm * norm)


def finish_call(keep, other):
    return call(finish_kernel, [((16, 2048), jnp.float32)], "vv", limit=4)(keep, other)[0]


def permute(x, pairs):
    return lax.ppermute(x, AXES, pairs)


def body(features, row_salt, column_multiplier, column_offset, thresholds):
    salt = row_salt.reshape(1, 128)
    params = [a.reshape(128, 128) for a in (column_multiplier, column_offset, thresholds)]
    partner = [(i, i ^ 8) for i in range(128)]
    other_salt = permute(salt, partner)
    xq, x0s, xa, x0k, xb, mine, queries = cast_call(features)
    yq = permute(xq, partner)
    y0s = permute(x0s, partner)
    ya = permute(xa, partner)
    y0k = permute(x0k, partner)
    yb = permute(xb, partner)
    own0s, own12 = own_call(mine, salt, *params)
    q, salts, sq_query = query_call(queries, yq, salt, other_salt, *params)
    common = (q, salts, *params)

    def gram(slot, kernel, outs, count, *operands):
        return gram_call(slot, kernel, outs, count, operands)

    send, keep = {}, {}
    (send[0, 0],) = gram(0, gram0s_first, 1, 2, own0s, y0s, *common)
    send[0, 1], keep[0, 1] = gram(1, gram1_first, 2, 4, own12, ya, *common)
    send[0, 2], keep[0, 2] = gram(
        2, gram2_first, 2, 4, own12, ya, *common, mine, y0s, y0k, sq_query
    )
    (send[1, 0],) = gram(0, gram0s_second, 1, 2, mine, yb, *common)
    send[1, 1], keep[1, 1] = gram(1, gram1_second, 2, 4, mine, yb, *common)
    send[1, 2], keep[1, 2] = gram(2, gram2_second, 2, 4, mine, yb, *common, sq_query)
    (keep[0, 0],) = gram(0, gram0k_first, 1, 2, mine, y0k, *common)
    (keep[1, 0],) = gram(0, gram0k_second, 1, 2, mine, yb, *common)
    none = [0, 0, 0]
    for step in range(2):
        rows = 8 >> step
        for half, slot in TURNS:
            turn = half, slot
            pairs = moves(axis_bits(slot + step), none)
            got = permute(send[turn], pairs)
            kept = keep[turn]
            send[turn] = kept[rows:] + got[rows:]
            keep[turn] = kept[:rows] + got[:rows]
    third = {}
    for half, slot in TURNS:
        pairs = moves(axis_bits(slot + 2), none)
        third[half, slot] = permute(send[half, slot], pairs)
    chunks = {}
    for half in (0, 1):
        keeps = [keep[half, slot] for slot in range(3)]
        gots = [third[half, slot] for slot in range(3)]
        joined = join_call(keeps, gots)
        for at in range(4):
            chunks[half + 2 * (at & 1) + 4 * (at >> 1)] = joined[at]
    parts = [chunks[0]]
    for j in LAST:
        parts.append(permute(chunks[j], moves(none, [j & 1, j >> 1 & 1, j >> 2])))
    send, keep = last_sum_call(parts)
    return finish_call(keep, permute(send, partner))


LAST = (6, 4, 2, 7, 5, 3, 1)
TURNS = [(half, slot) for half in (0, 1) for slot in range(3)]


def solution(mesh):
    placed = (P(AXES, None), P(AXES), P(), P(), P())
    return jax.shard_map(
        body, mesh=mesh, in_specs=placed, out_specs=P("rows", "tiles"), check_vma=False
    )
```

profile of v0, /device:TPU:1, one launch (start us, length us, event | category | flops | bytes accessed | tf_op | source)
XLA Modules:
  0.0 90.0 jit_solution(6577451315470201650)
XLA Ops:
  0.0 2.4 %shard_map.55 = (f32[128,256]{1,0:T(8,128)S(1)}, f32[2,128,384]{2,1,0:T(8,128)S(1)}, f32[4,128,640]{2,1,0:T(8,128)S(1)}, f32[2,128,384]{2,1,0:T(8,128)S(1)}, f32...) custom-call(bf16[128,16384]{1,0:T(8,128)(2,1)} %feat.1), custom_call_target="tpu_custom_call" | custom-call | flops 1000000 | bytes 6291456 | tf_op jit(solution)/shard_map/pallas_call | solution.py:115
  2.4 1.4 %collective-permute-start.6 = (f32[4,128,640]{2,1,0:T(8,128)S(1)}, f32[4,128,640]{2,1,0:T(8,128)S(1)}, u32[]{:S(2)}, u32[]{:S(2)}) collective-permute-start(f32[4,128,640]{2,1,0:T(8,128)S(1)} %get-tuple-element.44), channel_id=1, source_target_pairs={{0,8},{1,9},{2,10},{3,11},{4,12},{5,13},{6,14},{7,15},{8,0},{9,1},... | collective-permute-start | bytes 3932168 | tf_op jit(solution)/shard_map/ppermute | solution.py:405
  4.9 5.4 %collective-permute-done.2.other_salt = s32[1,128]{1,0:T(1,128)S(1)} collective-permute-done((s32[1,128]{1,0:T(1,128)S(1)}, s32[1,128]{1,0:T(1,128)S(1)}, u32[]{:S(2)}, u32[]{:S(2)}) %collective-permute-start.2) | collective-permute-done | bytes 544 | tf_op jit(solution)/shard_map/ppermute | solution.py:405
  10.6 0.9 shard_map.58
  11.8 0.5 shard_map.59
  12.3 2.7 %collective-permute-start.4 = (f32[16,96,128]{2,1,0:T(8,128)S(1)}, f32[16,96,128]{2,1,0:T(8,128)S(1)}, u32[]{:S(2)}, u32[]{:S(2)}) collective-permute-start(f32[16,96,128]{2,1,0:T(8,128)S(1)} %shard_map.59), channel_id=1, source_target_pairs={{0,1},{1,0},{2,3},{3,2},{4,5},{5,4},{6,7},{7,6},{8,11},{9,10},{10,... | collective-permute-start | bytes 2359304 | tf_op jit(solution)/shard_map/ppermute | solution.py:405
  15.0 0.9 %shard_map.61 = (f32[16,80,128]{2,1,0:T(8,128)S(1)}, f32[16,80,128]{2,1,0:T(8,128)S(1)}) custom-call(bf16[4,128,640]{2,1,0:T(8,128)(2,1)S(1)} %get-tuple-element.43.own, f32[4,128,640]{2,1,0:T(8,128)S(1)} %collective-permute-done.6.other, bf16[2,256,256]{2,1,0:T(8,128)(2,1)S(1)} %get-tuple-element.39.q, s32[256,128]{1,0:T(8,128)S(1)} %get-tuple-element.40.salt, ...), custom_call_target="tpu_custom_call" | custom-call | flops 128000000 | bytes 3145728 | tf_op jit(solution)/shard_map/pallas_call | solution.py:332
  15.9 1.7 %collective-permute-start.9 = (f32[16,80,128]{2,1,0:T(8,128)S(1)}, f32[16,80,128]{2,1,0:T(8,128)S(1)}, u32[]{:S(2)}, u32[]{:S(2)}) collective-permute-start(f32[16,80,128]{2,1,0:T(8,128)S(1)} %get-tuple-element.49), channel_id=1, source_target_pairs={{0,48},{1,49},{2,50},{3,51},{4,52},{5,53},{6,54},{7,55},{8,24},{9,... | collective-permute-start | bytes 1966088 | tf_op jit(solution)/shard_map/ppermute | solution.py:405
  17.6 0.7 shard_map.60
  18.3 1.4 %collective-permute-start.7 = (f32[16,96,128]{2,1,0:T(8,128)S(1)}, f32[16,96,128]{2,1,0:T(8,128)S(1)}, u32[]{:S(2)}, u32[]{:S(2)}) collective-permute-start(f32[16,96,128]{2,1,0:T(8,128)S(1)} %get-tuple-element.46), channel_id=1, source_target_pairs={{0,68},{1,69},{2,70},{3,71},{4,64},{5,65},{6,66},{7,67},{8,12},{9,... | collective-permute-start | bytes 2359304 | tf_op jit(solution)/shard_map/ppermute | solution.py:405
  19.7 0.6 shard_map.57
  20.3 4.3 %collective-permute-done.4 = f32[16,96,128]{2,1,0:T(8,128)S(1)} collective-permute-done((f32[16,96,128]{2,1,0:T(8,128)S(1)}, f32[16,96,128]{2,1,0:T(8,128)S(1)}, u32[]{:S(2)}, u32[]{:S(2)}) %collective-permute-start.4) | collective-permute-done | bytes 786464 | tf_op jit(solution)/shard_map/ppermute | solution.py:405
  24.8 1.5 %collective-permute-start.5 = (f32[8,96,128]{2,1,0:T(8,128)S(1)}, f32[8,96,128]{2,1,0:T(8,128)S(1)}, u32[]{:S(2)}, u32[]{:S(2)}) collective-permute-start(f32[8,96,128]{2,1,0:T(8,128)S(1)} %get-tuple-element.72), channel_id=1, source_target_pairs={{0,68},{1,69},{2,70},{3,71},{4,64},{5,65},{6,66},{7,67},{8,12},{9,... | collective-permute-start | bytes 1179656 | tf_op jit(solution)/shard_map/ppermute | solution.py:405
  26.4 2.6 %collective-permute-start.10 = (f32[8,80,128]{2,1,0:T(8,128)S(1)}, f32[8,80,128]{2,1,0:T(8,128)S(1)}, u32[]{:S(2)}, u32[]{:S(2)}) collective-permute-start(f32[8,80,128]{2,1,0:T(8,128)S(1)} %get-tuple-element.76), channel_id=1, source_target_pairs={{0,1},{1,0},{2,3},{3,2},{4,5},{5,4},{6,7},{7,6},{8,11},{9,10},{10,... | collective-permute-start | bytes 983048 | tf_op jit(solution)/shard_map/ppermute | solution.py:405
  29.0 1.1 %shard_map.65 = (f32[16,96,128]{2,1,0:T(8,128)S(1)}, f32[16,96,128]{2,1,0:T(8,128)S(1)}) custom-call(bf16[8,128,1024]{2,1,0:T(8,128)(2,1)S(1)} %get-tuple-element.35.mine, f32[4,128,1024]{2,1,0:T(8,128)S(1)} %collective-permute-done.17.other, bf16[2,256,256]{2,1,0:T(8,128)(2,1)S(1)} %get-tuple-element.39.q, s32[256,128]{1,0:T(8,128)S(1)} %get-tuple-element.40.salt, ...), custom_call_target="tpu_custom_call" | custom-call | flops 192000000 | bytes 3145728 | tf_op jit(solution)/shard_map/pallas_call | solution.py:332
  30.3 0.6 shard_map.64
  31.0 0.9 %collective-permute-start.18 = (f32[16,96,128]{2,1,0:T(8,128)S(1)}, f32[16,96,128]{2,1,0:T(8,128)S(1)}, u32[]{:S(2)}, u32[]{:S(2)}) collective-permute-start(f32[16,96,128]{2,1,0:T(8,128)S(1)} %shard_map.64), channel_id=1, source_target_pairs={{0,1},{1,0},{2,3},{3,2},{4,5},{5,4},{6,7},{7,6},{8,11},{9,10},{10,... | collective-permute-start | bytes 2359304 | tf_op jit(solution)/shard_map/ppermute | solution.py:405
  32.0 1.5 %collective-permute-start.8 = (f32[8,96,128]{2,1,0:T(8,128)S(1)}, f32[8,96,128]{2,1,0:T(8,128)S(1)}, u32[]{:S(2)}, u32[]{:S(2)}) collective-permute-start(f32[8,96,128]{2,1,0:T(8,128)S(1)} %get-tuple-element.70), channel_id=1, source_target_pairs={{0,48},{1,49},{2,50},{3,51},{4,52},{5,53},{6,54},{7,55},{8,24},{9,... | collective-permute-start | bytes 1179656 | tf_op jit(solution)/shard_map/ppermute | solution.py:405
  33.9 0.6 shard_map.63
  34.5 1.2 %shard_map.66 = (f32[16,80,128]{2,1,0:T(8,128)S(1)}, f32[16,80,128]{2,1,0:T(8,128)S(1)}) custom-call(bf16[8,128,1024]{2,1,0:T(8,128)(2,1)S(1)} %get-tuple-element.35.mine, f32[4,128,1024]{2,1,0:T(8,128)S(1)} %collective-permute-done.17.other, bf16[2,256,256]{2,1,0:T(8,128)(2,1)S(1)} %get-tuple-element.39.q, s32[256,128]{1,0:T(8,128)S(1)} %get-tuple-element.40.salt, ...), custom_call_target="tpu_custom_call" | custom-call | flops 128000000 | bytes 3145728 | tf_op jit(solution)/shard_map/pallas_call | solution.py:332
  35.8 1.5 %collective-permute-start.22 = (f32[16,80,128]{2,1,0:T(8,128)S(1)}, f32[16,80,128]{2,1,0:T(8,128)S(1)}, u32[]{:S(2)}, u32[]{:S(2)}) collective-permute-start(f32[16,80,128]{2,1,0:T(8,128)S(1)} %get-tuple-element.58), channel_id=1, source_target_pairs={{0,48},{1,49},{2,50},{3,51},{4,52},{5,53},{6,54},{7,55},{8,24},{9,... | collective-permute-start | bytes 1966088 | tf_op jit(solution)/shard_map/ppermute | solution.py:405
  37.3 1.7 %collective-permute-done.8 = f32[8,96,128]{2,1,0:T(8,128)S(1)} collective-permute-done((f32[8,96,128]{2,1,0:T(8,128)S(1)}, f32[8,96,128]{2,1,0:T(8,128)S(1)}, u32[]{:S(2)}, u32[]{:S(2)}) %collective-permute-start.8) | collective-permute-done | bytes 393248 | tf_op jit(solution)/shard_map/ppermute | solution.py:405
  39.0 0.6 collective-permute-start.13
  39.7 2.5 %collective-permute-done.20 = f32[16,96,128]{2,1,0:T(8,128)S(1)} collective-permute-done((f32[16,96,128]{2,1,0:T(8,128)S(1)}, f32[16,96,128]{2,1,0:T(8,128)S(1)}, u32[]{:S(2)}, u32[]{:S(2)}) %collective-permute-start.20) | collective-permute-done | bytes 786464 | tf_op jit(solution)/shard_map/ppermute | solution.py:405
  42.2 0.7 collective-permute-start.12
  43.4 1.6 %collective-permute-start.21 = (f32[8,96,128]{2,1,0:T(8,128)S(1)}, f32[8,96,128]{2,1,0:T(8,128)S(1)}, u32[]{:S(2)}, u32[]{:S(2)}) collective-permute-start(f32[8,96,128]{2,1,0:T(8,128)S(1)} %get-tuple-element.66), channel_id=1, source_target_pairs={{0,48},{1,49},{2,50},{3,51},{4,52},{5,53},{6,54},{7,55},{8,24},{9,... | collective-permute-start | bytes 1179656 | tf_op jit(solution)/shard_map/ppermute | solution.py:405
  45.1 3.1 %collective-permute-done.22 = f32[16,80,128]{2,1,0:T(8,128)S(1)} collective-permute-done((f32[16,80,128]{2,1,0:T(8,128)S(1)}, f32[16,80,128]{2,1,0:T(8,128)S(1)}, u32[]{:S(2)}, u32[]{:S(2)}) %collective-permute-start.22) | collective-permute-done | bytes 655392 | tf_op jit(solution)/shard_map/ppermute | solution.py:405
  48.2 0.6 collective-permute-start.19
  48.9 3.5 %collective-permute-done.21 = f32[8,96,128]{2,1,0:T(8,128)S(1)} collective-permute-done((f32[8,96,128]{2,1,0:T(8,128)S(1)}, f32[8,96,128]{2,1,0:T(8,128)S(1)}, u32[]{:S(2)}, u32[]{:S(2)}) %collective-permute-start.21) | collective-permute-done | bytes 393248 | tf_op jit(solution)/shard_map/ppermute | solution.py:405
  52.4 2.0 %collective-permute-start.23 = (f32[8,80,128]{2,1,0:T(8,128)S(1)}, f32[8,80,128]{2,1,0:T(8,128)S(1)}, u32[]{:S(2)}, u32[]{:S(2)}) collective-permute-start(f32[8,80,128]{2,1,0:T(8,128)S(1)} %get-tuple-element.74), channel_id=1, source_target_pairs={{0,1},{1,0},{2,3},{3,2},{4,5},{5,4},{6,7},{7,6},{8,11},{9,10},{10,... | collective-permute-start | bytes 983048 | tf_op jit(solution)/shard_map/ppermute | solution.py:405
  54.4 0.7 collective-permute-done.19
  55.1 2.0 %collective-permute-start.25 = (f32[4,96,128]{2,1,0:T(8,128)S(1)}, f32[4,96,128]{2,1,0:T(8,128)S(1)}, u32[]{:S(2)}, u32[]{:S(2)}) collective-permute-start(f32[4,96,128]{2,1,0:T(8,128)S(1)} %get-tuple-element.77), channel_id=1, source_target_pairs={{0,1},{1,0},{2,3},{3,2},{4,5},{5,4},{6,7},{7,6},{8,11},{9,10},{10,... | collective-permute-start | bytes 589832 | tf_op jit(solution)/shard_map/ppermute | solution.py:405
  57.1 2.7 %collective-permute-done.23 = f32[8,80,128]{2,1,0:T(8,128)S(1)} collective-permute-done((f32[8,80,128]{2,1,0:T(8,128)S(1)}, f32[8,80,128]{2,1,0:T(8,128)S(1)}, u32[]{:S(2)}, u32[]{:S(2)}) %collective-permute-start.23) | collective-permute-done | bytes 327712 | tf_op jit(solution)/shard_map/ppermute | solution.py:405
  59.8 1.2 %collective-permute-start.24 = (f32[4,96,128]{2,1,0:T(8,128)S(1)}, f32[4,96,128]{2,1,0:T(8,128)S(1)}, u32[]{:S(2)}, u32[]{:S(2)}) collective-permute-start(f32[4,96,128]{2,1,0:T(8,128)S(1)} %get-tuple-element.79), channel_id=1, source_target_pairs={{0,48},{1,49},{2,50},{3,51},{4,52},{5,53},{6,54},{7,55},{8,24},{9,... | collective-permute-start | bytes 589832 | tf_op jit(solution)/shard_map/ppermute | solution.py:405
  61.0 0.6 collective-permute-start.26
  61.7 4.4 %collective-permute-start.14 = (f32[272,128]{1,0:T(8,128)S(1)}, f32[272,128]{1,0:T(8,128)S(1)}, u32[]{:S(2)}, u32[]{:S(2)}) collective-permute-start(f32[272,128]{1,0:T(8,128)S(1)} %get-tuple-element.51), channel_id=1, source_target_pairs={{0,20},{1,21},{2,22},{3,23},{4,16},{5,17},{6,18},{7,19},{8,124},{9... | collective-permute-start | bytes 417800 | tf_op jit(solution)/shard_map/ppermute | solution.py:405
  66.1 0.4 collective-permute-start.15
  66.6 1.2 %collective-permute-start.16 = (f32[272,128]{1,0:T(8,128)S(1)}, f32[272,128]{1,0:T(8,128)S(1)}, u32[]{:S(2)}, u32[]{:S(2)}) collective-permute-start(f32[272,128]{1,0:T(8,128)S(1)} %get-tuple-element.53), channel_id=1, source_target_pairs={{0,4},{1,5},{2,6},{3,7},{4,0},{5,1},{6,2},{7,3},{8,76},{9,77},{10,... | collective-permute-start | bytes 417800 | tf_op jit(solution)/shard_map/ppermute | solution.py:405
  67.9 1.0 %collective-permute-start.27 = (f32[272,128]{1,0:T(8,128)S(1)}, f32[272,128]{1,0:T(8,128)S(1)}, u32[]{:S(2)}, u32[]{:S(2)}) collective-permute-start(f32[272,128]{1,0:T(8,128)S(1)} %get-tuple-element.59), channel_id=1, source_target_pairs={{0,23},{1,22},{2,21},{3,20},{4,19},{5,18},{6,17},{7,16},{8,125},{9... | collective-permute-start | bytes 417800 | tf_op jit(solution)/shard_map/ppermute | solution.py:405
  68.9 3.8 %collective-permute-start.28 = (f32[272,128]{1,0:T(8,128)S(1)}, f32[272,128]{1,0:T(8,128)S(1)}, u32[]{:S(2)}, u32[]{:S(2)}) collective-permute-start(f32[272,128]{1,0:T(8,128)S(1)} %get-tuple-element.60), channel_id=1, source_target_pairs={{0,19},{1,18},{2,17},{3,16},{4,23},{5,22},{6,21},{7,20},{8,57},{9,... | collective-permute-start | bytes 417800 | tf_op jit(solution)/shard_map/ppermute | solution.py:405
  72.7 0.9 %collective-permute-start.29 = (f32[272,128]{1,0:T(8,128)S(1)}, f32[272,128]{1,0:T(8,128)S(1)}, u32[]{:S(2)}, u32[]{:S(2)}) collective-permute-start(f32[272,128]{1,0:T(8,128)S(1)} %get-tuple-element.61), channel_id=1, source_target_pairs={{0,7},{1,6},{2,5},{3,4},{4,3},{5,2},{6,1},{7,0},{8,77},{9,76},{10,... | collective-permute-start | bytes 417800 | tf_op jit(solution)/shard_map/ppermute | solution.py:405
  73.6 1.5 %collective-permute-start.30 = (f32[272,128]{1,0:T(8,128)S(1)}, f32[272,128]{1,0:T(8,128)S(1)}, u32[]{:S(2)}, u32[]{:S(2)}) collective-permute-start(f32[272,128]{1,0:T(8,128)S(1)} %get-tuple-element.62), channel_id=1, source_target_pairs={{0,3},{1,2},{2,1},{3,0},{4,7},{5,6},{6,5},{7,4},{8,9},{9,8},{10,11... | collective-permute-start | bytes 417800 | tf_op jit(solution)/shard_map/ppermute | solution.py:405
  75.1 1.9 %collective-permute-done.27.refs_4_ = f32[272,128]{1,0:T(8,128)S(1)} collective-permute-done((f32[272,128]{1,0:T(8,128)S(1)}, f32[272,128]{1,0:T(8,128)S(1)}, u32[]{:S(2)}, u32[]{:S(2)}) %collective-permute-start.27) | collective-permute-done | bytes 139296 | tf_op jit(solution)/shard_map/ppermute | solution.py:405
  77.1 0.5 collective-permute-done.28.refs_5_
  77.6 1.9 %collective-permute-done.29.refs_6_ = f32[272,128]{1,0:T(8,128)S(1)} collective-permute-done((f32[272,128]{1,0:T(8,128)S(1)}, f32[272,128]{1,0:T(8,128)S(1)}, u32[]{:S(2)}, u32[]{:S(2)}) %collective-permute-start.29) | collective-permute-done | bytes 139296 | tf_op jit(solution)/shard_map/ppermute | solution.py:405
  80.0 8.3 %collective-permute-start.31 = (f32[136,128]{1,0:T(8,128)S(1)}, f32[136,128]{1,0:T(8,128)S(1)}, u32[]{:S(2)}, u32[]{:S(2)}) collective-permute-start(f32[136,128]{1,0:T(8,128)S(1)} %get-tuple-element.64), channel_id=1, source_target_pairs={{0,8},{1,9},{2,10},{3,11},{4,12},{5,13},{6,14},{7,15},{8,0},{9,1},... | collective-permute-start | bytes 208904 | tf_op jit(solution)/shard_map/ppermute | solution.py:405
  88.3 0.9 %collective-permute-done.31.other = f32[136,128]{1,0:T(8,128)S(1)} collective-permute-done((f32[136,128]{1,0:T(8,128)S(1)}, f32[136,128]{1,0:T(8,128)S(1)}, u32[]{:S(2)}, u32[]{:S(2)}) %collective-permute-start.31) | collective-permute-done | bytes 69664 | tf_op jit(solution)/shard_map/ppermute | solution.py:405
  89.3 0.8 shard_map.69
  (51 shorter events, 4.2 us)
Async XLA Ops:
  0.0 4.5 %copy-start.3 = (s32[128]{0:T(128)S(1)}, s32[128]{0:T(128)}, u32[]{:S(2)}) copy-start(s32[128]{0:T(128)} %param.6) | copy-start | bytes 1540
  0.0 10.6 %copy-start = (s32[16384]{0:T(1024)S(1)}, s32[16384]{0:T(1024)}, u32[]{:S(2)}) copy-start(s32[16384]{0:T(1024)} %param.7) | copy-start | bytes 196612
  0.0 10.6 %copy-start.1 = (s32[16384]{0:T(1024)S(1)}, s32[16384]{0:T(1024)}, u32[]{:S(2)}) copy-start(s32[16384]{0:T(1024)} %param.8) | copy-start | bytes 196612
  0.0 10.6 %copy-start.2 = (s32[16384]{0:T(1024)S(1)}, s32[16384]{0:T(1024)}, u32[]{:S(2)}) copy-start(s32[16384]{0:T(1024)} %param.9) | copy-start | bytes 196612
  2.4 12.6 %collective-permute-start.6 = (f32[4,128,640]{2,1,0:T(8,128)S(1)}, f32[4,128,640]{2,1,0:T(8,128)S(1)}, u32[]{:S(2)}, u32[]{:S(2)}) collective-permute-start(f32[4,128,640]{2,1,0:T(8,128)S(1)} %get-tuple-element.44), channel_id=1, source_target_pairs={{0,8},{1,9},{2,10},{3,11},{4,12},{5,13},{6,14},{7,15},{8,0},{9,1},... | collective-permute-start | bytes 3932168 | tf_op jit(solution)/shard_map/ppermute | solution.py:405
  3.9 25.1 %collective-permute-start.17 = (f32[4,128,1024]{2,1,0:T(8,128)S(1)}, f32[4,128,1024]{2,1,0:T(8,128)S(1)}, u32[]{:S(2)}, u32[]{:S(2)}) collective-permute-start(f32[4,128,1024]{2,1,0:T(8,128)S(1)} %get-tuple-element.54), channel_id=1, source_target_pairs={{0,8},{1,9},{2,10},{3,11},{4,12},{5,13},{6,14},{7,15},{8,0},{9,1},... | collective-permute-start | bytes 6291464 | tf_op jit(solution)/shard_map/ppermute | solution.py:405
  3.9 7.9 %collective-permute-start.3 = (f32[2,128,384]{2,1,0:T(8,128)S(1)}, f32[2,128,384]{2,1,0:T(8,128)S(1)}, u32[]{:S(2)}, u32[]{:S(2)}) collective-permute-start(f32[2,128,384]{2,1,0:T(8,128)S(1)} %get-tuple-element.42), channel_id=1, source_target_pairs={{0,8},{1,9},{2,10},{3,11},{4,12},{5,13},{6,14},{7,15},{8,0},{9,1},... | collective-permute-start | bytes 1179656 | tf_op jit(solution)/shard_map/ppermute | solution.py:405
  4.4 7.1 %collective-permute-start.1 = (f32[128,256]{1,0:T(8,128)S(1)}, f32[128,256]{1,0:T(8,128)S(1)}, u32[]{:S(2)}, u32[]{:S(2)}) collective-permute-start(f32[128,256]{1,0:T(8,128)S(1)} %get-tuple-element.38), channel_id=1, source_target_pairs={{0,8},{1,9},{2,10},{3,11},{4,12},{5,13},{6,14},{7,15},{8,0},{9,1},... | collective-permute-start | bytes 393224 | tf_op jit(solution)/shard_map/ppermute | solution.py:405
  4.5 5.8 %collective-permute-start.2 = (s32[1,128]{1,0:T(1,128)S(1)}, s32[1,128]{1,0:T(1,128)S(1)}, u32[]{:S(2)}, u32[]{:S(2)}) collective-permute-start(s32[1,128]{1,0:T(1,128)S(1)} %bitcast.34), channel_id=1, source_target_pairs={{0,8},{1,9},{2,10},{3,11},{4,12},{5,13},{6,14},{7,15},{8,0},{9,1},... | collective-permute-start | bytes 1544 | tf_op jit(solution)/shard_map/ppermute | solution.py:405
  10.3 4.7 %collective-permute-start = (f32[2,128,384]{2,1,0:T(8,128)S(1)}, f32[2,128,384]{2,1,0:T(8,128)S(1)}, u32[]{:S(2)}, u32[]{:S(2)}) collective-permute-start(f32[2,128,384]{2,1,0:T(8,128)S(1)} %get-tuple-element.36), channel_id=1, source_target_pairs={{0,8},{1,9},{2,10},{3,11},{4,12},{5,13},{6,14},{7,15},{8,0},{9,1},... | collective-permute-start | bytes 1179656 | tf_op jit(solution)/shard_map/ppermute | solution.py:405
  12.3 12.4 %collective-permute-start.4 = (f32[16,96,128]{2,1,0:T(8,128)S(1)}, f32[16,96,128]{2,1,0:T(8,128)S(1)}, u32[]{:S(2)}, u32[]{:S(2)}) collective-permute-start(f32[16,96,128]{2,1,0:T(8,128)S(1)} %shard_map.59), channel_id=1, source_target_pairs={{0,1},{1,0},{2,3},{3,2},{4,5},{5,4},{6,7},{7,6},{8,11},{9,10},{10,... | collective-permute-start | bytes 2359304 | tf_op jit(solution)/shard_map/ppermute | solution.py:405
  15.9 10.4 %collective-permute-start.9 = (f32[16,80,128]{2,1,0:T(8,128)S(1)}, f32[16,80,128]{2,1,0:T(8,128)S(1)}, u32[]{:S(2)}, u32[]{:S(2)}) collective-permute-start(f32[16,80,128]{2,1,0:T(8,128)S(1)} %get-tuple-element.49), channel_id=1, source_target_pairs={{0,48},{1,49},{2,50},{3,51},{4,52},{5,53},{6,54},{7,55},{8,24},{9,... | collective-permute-start | bytes 1966088 | tf_op jit(solution)/shard_map/ppermute | solution.py:405
  18.3 13.6 %collective-permute-start.7 = (f32[16,96,128]{2,1,0:T(8,128)S(1)}, f32[16,96,128]{2,1,0:T(8,128)S(1)}, u32[]{:S(2)}, u32[]{:S(2)}) collective-permute-start(f32[16,96,128]{2,1,0:T(8,128)S(1)} %get-tuple-element.46), channel_id=1, source_target_pairs={{0,68},{1,69},{2,70},{3,71},{4,64},{5,65},{6,66},{7,67},{8,12},{9,... | collective-permute-start | bytes 2359304 | tf_op jit(solution)/shard_map/ppermute | solution.py:405
  24.8 8.9 %collective-permute-start.5 = (f32[8,96,128]{2,1,0:T(8,128)S(1)}, f32[8,96,128]{2,1,0:T(8,128)S(1)}, u32[]{:S(2)}, u32[]{:S(2)}) collective-permute-start(f32[8,96,128]{2,1,0:T(8,128)S(1)} %get-tuple-element.72), channel_id=1, source_target_pairs={{0,68},{1,69},{2,70},{3,71},{4,64},{5,65},{6,66},{7,67},{8,12},{9,... | collective-permute-start | bytes 1179656 | tf_op jit(solution)/shard_map/ppermute | solution.py:405
  26.4 9.3 %collective-permute-start.10 = (f32[8,80,128]{2,1,0:T(8,128)S(1)}, f32[8,80,128]{2,1,0:T(8,128)S(1)}, u32[]{:S(2)}, u32[]{:S(2)}) collective-permute-start(f32[8,80,128]{2,1,0:T(8,128)S(1)} %get-tuple-element.76), channel_id=1, source_target_pairs={{0,1},{1,0},{2,3},{3,2},{4,5},{5,4},{6,7},{7,6},{8,11},{9,10},{10,... | collective-permute-start | bytes 983048 | tf_op jit(solution)/shard_map/ppermute | solution.py:405
  30.1 12.1 %collective-permute-start.20 = (f32[16,96,128]{2,1,0:T(8,128)S(1)}, f32[16,96,128]{2,1,0:T(8,128)S(1)}, u32[]{:S(2)}, u32[]{:S(2)}) collective-permute-start(f32[16,96,128]{2,1,0:T(8,128)S(1)} %get-tuple-element.56), channel_id=1, source_target_pairs={{0,68},{1,69},{2,70},{3,71},{4,64},{5,65},{6,66},{7,67},{8,12},{9,... | collective-permute-start | bytes 2359304 | tf_op jit(solution)/shard_map/ppermute | solution.py:405
  31.0 12.4 %collective-permute-start.18 = (f32[16,96,128]{2,1,0:T(8,128)S(1)}, f32[16,96,128]{2,1,0:T(8,128)S(1)}, u32[]{:S(2)}, u32[]{:S(2)}) collective-permute-start(f32[16,96,128]{2,1,0:T(8,128)S(1)} %shard_map.64), channel_id=1, source_target_pairs={{0,1},{1,0},{2,3},{3,2},{4,5},{5,4},{6,7},{7,6},{8,11},{9,10},{10,... | collective-permute-start | bytes 2359304 | tf_op jit(solution)/shard_map/ppermute | solution.py:405
  32.0 7.0 %collective-permute-start.8 = (f32[8,96,128]{2,1,0:T(8,128)S(1)}, f32[8,96,128]{2,1,0:T(8,128)S(1)}, u32[]{:S(2)}, u32[]{:S(2)}) collective-permute-start(f32[8,96,128]{2,1,0:T(8,128)S(1)} %get-tuple-element.70), channel_id=1, source_target_pairs={{0,48},{1,49},{2,50},{3,51},{4,52},{5,53},{6,54},{7,55},{8,24},{9,... | collective-permute-start | bytes 1179656 | tf_op jit(solution)/shard_map/ppermute | solution.py:405
  33.8 27.2 %collective-permute-start.11 = (f32[4,96,128]{2,1,0:T(8,128)S(1)}, f32[4,96,128]{2,1,0:T(8,128)S(1)}, u32[]{:S(2)}, u32[]{:S(2)}) collective-permute-start(f32[4,96,128]{2,1,0:T(8,128)S(1)} %get-tuple-element.83), channel_id=1, source_target_pairs={{0,48},{1,49},{2,50},{3,51},{4,52},{5,53},{6,54},{7,55},{8,24},{9,... | collective-permute-start | bytes 589832 | tf_op jit(solution)/shard_map/ppermute | solution.py:405
  35.8 12.4 %collective-permute-start.22 = (f32[16,80,128]{2,1,0:T(8,128)S(1)}, f32[16,80,128]{2,1,0:T(8,128)S(1)}, u32[]{:S(2)}, u32[]{:S(2)}) collective-permute-start(f32[16,80,128]{2,1,0:T(8,128)S(1)} %get-tuple-element.58), channel_id=1, source_target_pairs={{0,48},{1,49},{2,50},{3,51},{4,52},{5,53},{6,54},{7,55},{8,24},{9,... | collective-permute-start | bytes 1966088 | tf_op jit(solution)/shard_map/ppermute | solution.py:405
  39.0 22.6 %collective-permute-start.13 = (f32[4,80,128]{2,1,0:T(8,128)S(1)}, f32[4,80,128]{2,1,0:T(8,128)S(1)}, u32[]{:S(2)}, u32[]{:S(2)}) collective-permute-start(f32[4,80,128]{2,1,0:T(8,128)S(1)} %get-tuple-element.87), channel_id=1, source_target_pairs={{0,68},{1,69},{2,70},{3,71},{4,64},{5,65},{6,66},{7,67},{8,12},{9,... | collective-permute-start | bytes 491528 | tf_op jit(solution)/shard_map/ppermute | solution.py:405
  42.2 19.4 %collective-permute-start.12 = (f32[4,96,128]{2,1,0:T(8,128)S(1)}, f32[4,96,128]{2,1,0:T(8,128)S(1)}, u32[]{:S(2)}, u32[]{:S(2)}) collective-permute-start(f32[4,96,128]{2,1,0:T(8,128)S(1)} %get-tuple-element.81), channel_id=1, source_target_pairs={{0,1},{1,0},{2,3},{3,2},{4,5},{5,4},{6,7},{7,6},{8,11},{9,10},{10,... | collective-permute-start | bytes 589832 | tf_op jit(solution)/shard_map/ppermute | solution.py:405
  43.4 9.0 %collective-permute-start.21 = (f32[8,96,128]{2,1,0:T(8,128)S(1)}, f32[8,96,128]{2,1,0:T(8,128)S(1)}, u32[]{:S(2)}, u32[]{:S(2)}) collective-permute-start(f32[8,96,128]{2,1,0:T(8,128)S(1)} %get-tuple-element.66), channel_id=1, source_target_pairs={{0,48},{1,49},{2,50},{3,51},{4,52},{5,53},{6,54},{7,55},{8,24},{9,... | collective-permute-start | bytes 1179656 | tf_op jit(solution)/shard_map/ppermute | solution.py:405
  48.2 6.9 %collective-permute-start.19 = (f32[8,96,128]{2,1,0:T(8,128)S(1)}, f32[8,96,128]{2,1,0:T(8,128)S(1)}, u32[]{:S(2)}, u32[]{:S(2)}) collective-permute-start(f32[8,96,128]{2,1,0:T(8,128)S(1)} %get-tuple-element.68), channel_id=1, source_target_pairs={{0,68},{1,69},{2,70},{3,71},{4,64},{5,65},{6,66},{7,67},{8,12},{9,... | collective-permute-start | bytes 1179656 | tf_op jit(solution)/shard_map/ppermute | solution.py:405
  52.4 7.4 %collective-permute-start.23 = (f32[8,80,128]{2,1,0:T(8,128)S(1)}, f32[8,80,128]{2,1,0:T(8,128)S(1)}, u32[]{:S(2)}, u32[]{:S(2)}) collective-permute-start(f32[8,80,128]{2,1,0:T(8,128)S(1)} %get-tuple-element.74), channel_id=1, source_target_pairs={{0,1},{1,0},{2,3},{3,2},{4,5},{5,4},{6,7},{7,6},{8,11},{9,10},{10,... | collective-permute-start | bytes 983048 | tf_op jit(solution)/shard_map/ppermute | solution.py:405
  55.1 12.7 %collective-permute-start.25 = (f32[4,96,128]{2,1,0:T(8,128)S(1)}, f32[4,96,128]{2,1,0:T(8,128)S(1)}, u32[]{:S(2)}, u32[]{:S(2)}) collective-permute-start(f32[4,96,128]{2,1,0:T(8,128)S(1)} %get-tuple-element.77), channel_id=1, source_target_pairs={{0,1},{1,0},{2,3},{3,2},{4,5},{5,4},{6,7},{7,6},{8,11},{9,10},{10,... | collective-permute-start | bytes 589832 | tf_op jit(solution)/shard_map/ppermute | solution.py:405
  59.8 8.0 %collective-permute-start.24 = (f32[4,96,128]{2,1,0:T(8,128)S(1)}, f32[4,96,128]{2,1,0:T(8,128)S(1)}, u32[]{:S(2)}, u32[]{:S(2)}) collective-permute-start(f32[4,96,128]{2,1,0:T(8,128)S(1)} %get-tuple-element.79), channel_id=1, source_target_pairs={{0,48},{1,49},{2,50},{3,51},{4,52},{5,53},{6,54},{7,55},{8,24},{9,... | collective-permute-start | bytes 589832 | tf_op jit(solution)/shard_map/ppermute | solution.py:405
  61.0 5.5 %collective-permute-start.26 = (f32[4,80,128]{2,1,0:T(8,128)S(1)}, f32[4,80,128]{2,1,0:T(8,128)S(1)}, u32[]{:S(2)}, u32[]{:S(2)}) collective-permute-start(f32[4,80,128]{2,1,0:T(8,128)S(1)} %get-tuple-element.85), channel_id=1, source_target_pairs={{0,68},{1,69},{2,70},{3,71},{4,64},{5,65},{6,66},{7,67},{8,12},{9,... | collective-permute-start | bytes 491528 | tf_op jit(solution)/shard_map/ppermute | solution.py:405
  61.7 11.0 %collective-permute-start.14 = (f32[272,128]{1,0:T(8,128)S(1)}, f32[272,128]{1,0:T(8,128)S(1)}, u32[]{:S(2)}, u32[]{:S(2)}) collective-permute-start(f32[272,128]{1,0:T(8,128)S(1)} %get-tuple-element.51), channel_id=1, source_target_pairs={{0,20},{1,21},{2,22},{3,23},{4,16},{5,17},{6,18},{7,19},{8,124},{9... | collective-permute-start | bytes 417800 | tf_op jit(solution)/shard_map/ppermute | solution.py:405
  66.1 7.5 %collective-permute-start.15 = (f32[272,128]{1,0:T(8,128)S(1)}, f32[272,128]{1,0:T(8,128)S(1)}, u32[]{:S(2)}, u32[]{:S(2)}) collective-permute-start(f32[272,128]{1,0:T(8,128)S(1)} %get-tuple-element.52), channel_id=1, source_target_pairs={{0,16},{1,17},{2,18},{3,19},{4,20},{5,21},{6,22},{7,23},{8,56},{9,... | collective-permute-start | bytes 417800 | tf_op jit(solution)/shard_map/ppermute | solution.py:405
  66.6 8.6 %collective-permute-start.16 = (f32[272,128]{1,0:T(8,128)S(1)}, f32[272,128]{1,0:T(8,128)S(1)}, u32[]{:S(2)}, u32[]{:S(2)}) collective-permute-start(f32[272,128]{1,0:T(8,128)S(1)} %get-tuple-element.53), channel_id=1, source_target_pairs={{0,4},{1,5},{2,6},{3,7},{4,0},{5,1},{6,2},{7,3},{8,76},{9,77},{10,... | collective-permute-start | bytes 417800 | tf_op jit(solution)/shard_map/ppermute | solution.py:405
  67.9 9.2 %collective-permute-start.27 = (f32[272,128]{1,0:T(8,128)S(1)}, f32[272,128]{1,0:T(8,128)S(1)}, u32[]{:S(2)}, u32[]{:S(2)}) collective-permute-start(f32[272,128]{1,0:T(8,128)S(1)} %get-tuple-element.59), channel_id=1, source_target_pairs={{0,23},{1,22},{2,21},{3,20},{4,19},{5,18},{6,17},{7,16},{8,125},{9... | collective-permute-start | bytes 417800 | tf_op jit(solution)/shard_map/ppermute | solution.py:405
  68.9 8.7 %collective-permute-start.28 = (f32[272,128]{1,0:T(8,128)S(1)}, f32[272,128]{1,0:T(8,128)S(1)}, u32[]{:S(2)}, u32[]{:S(2)}) collective-permute-start(f32[272,128]{1,0:T(8,128)S(1)} %get-tuple-element.60), channel_id=1, source_target_pairs={{0,19},{1,18},{2,17},{3,16},{4,23},{5,22},{6,21},{7,20},{8,57},{9,... | collective-permute-start | bytes 417800 | tf_op jit(solution)/shard_map/ppermute | solution.py:405
  72.7 6.8 %collective-permute-start.29 = (f32[272,128]{1,0:T(8,128)S(1)}, f32[272,128]{1,0:T(8,128)S(1)}, u32[]{:S(2)}, u32[]{:S(2)}) collective-permute-start(f32[272,128]{1,0:T(8,128)S(1)} %get-tuple-element.61), channel_id=1, source_target_pairs={{0,7},{1,6},{2,5},{3,4},{4,3},{5,2},{6,1},{7,0},{8,77},{9,76},{10,... | collective-permute-start | bytes 417800 | tf_op jit(solution)/shard_map/ppermute | solution.py:405
  73.6 6.3 %collective-permute-start.30 = (f32[272,128]{1,0:T(8,128)S(1)}, f32[272,128]{1,0:T(8,128)S(1)}, u32[]{:S(2)}, u32[]{:S(2)}) collective-permute-start(f32[272,128]{1,0:T(8,128)S(1)} %get-tuple-element.62), channel_id=1, source_target_pairs={{0,3},{1,2},{2,1},{3,0},{4,7},{5,6},{6,5},{7,4},{8,9},{9,8},{10,11... | collective-permute-start | bytes 417800 | tf_op jit(solution)/shard_map/ppermute | solution.py:405
  80.0 9.2 %collective-permute-start.31 = (f32[136,128]{1,0:T(8,128)S(1)}, f32[136,128]{1,0:T(8,128)S(1)}, u32[]{:S(2)}, u32[]{:S(2)}) collective-permute-start(f32[136,128]{1,0:T(8,128)S(1)} %get-tuple-element.64), channel_id=1, source_target_pairs={{0,8},{1,9},{2,10},{3,11},{4,12},{5,13},{6,14},{7,15},{8,0},{9,1},... | collective-permute-start | bytes 208904 | tf_op jit(solution)/shard_map/ppermute | solution.py:405
where the time goes:
time: 90.1 us; the launch traced here: 90 us
  starting transfers between devices  48 us (53%)
  waiting for transfers between devices  30.2 us (34%)
  Pallas kernels  10.8 us (12%)
    ppermute x32, starting transfers between devices, permute(): return lax.ppermute(x, AXES, pairs)  48 us
    ppermute x32, waiting for transfers between devices, permute(): return lax.ppermute(x, AXES, pairs)  30.2 us
    pallas_call x8, Pallas kernels, gram_call(): call(kernel, [((16, SLOT_ROWS[slot], 128), jnp.float32)] * outs, 'v' * le...  6.28 us
    pallas_call x1, Pallas kernels, cast_call(): call(cast_kernel, [((128, 256), f32), ((2, 128, 384), f32), ((4, 128, 640...  2.39 us
  transfers between devices with their start and end apart: 32, of which 15 were waited for; matrix products, arithmetic and copies ran while one was open for 1% of the time, Pallas kernels for 8%

commit v1 on v0

--- a/solution.py
+++ b/solution.py
@@ -30,7 +30,7 @@
 def flip(index, first, last):
     chip, core = place(index)
     for axis in range(3):
-        kind = core if axis == 0 else 1 - core
+        kind = core if axis == 2 else 1 - core
         mask = first[axis] << kind | last[axis] << (1 - kind)
         chip[axis] = gray(gray(chip[axis]) ^ mask)
     return index_of(chip, core)
@@ -51,7 +51,7 @@
 
 
 def tile_at(core, tile, c, xa, xb):
-    high = jnp.where(core == 0, xb, xa)
+    high = jnp.where(core == 1, xb, xa)
     return tile ^ (c * 4 + high * 2 + (xa ^ xb))
 
 
@@ -196,7 +196,7 @@
     for c in range(2):
         for group in range(8):
             ya, za, zb = group >> 2, group >> 1 & 1, group & 1
-            z_high = jnp.where(core == 1, zb, za)
+            z_high = jnp.where(core == 0, zb, za)
             y_high = jnp.where(core == 1, c ^ ya, ya)
             at = pair ^ (y_high * 4 + z_high * 2 + (za ^ zb))
             start = pl.multiple_of(at * 32, 32)

time: 90.1 us -> 89.6 us (level)
  starting transfers between devices: 48 us -> 45.8 us
  waiting for transfers between devices: 30.2 us -> 31.8 us
    ppermute x32, starting transfers between devices: 48 us -> 45.8 us  [permute(): return lax.ppermute(x, AXES, pairs)]
    ppermute x32, waiting for transfers between devices: 30.2 us -> 31.8 us  [permute(): return lax.ppermute(x, AXES, pairs)]
  transfers between devices with their start and end apart: 32 -> 32, of which waited for: 15 -> 16; matrix products, arithmetic and copies ran while one was open for 1% -> 1% of each run, Pallas kernels for 8% -> 8%
where the time goes in v1:
time: 89.6 us; the launch traced here: 89.5 us
  starting transfers between devices  45.8 us (51%)
  waiting for transfers between devices  31.8 us (35%)
  Pallas kernels  10.8 us (12%)
    ppermute x32, starting transfers between devices, permute(): return lax.ppermute(x, AXES, pairs)  45.8 us
    ppermute x32, waiting for transfers between devices, permute(): return lax.ppermute(x, AXES, pairs)  31.8 us
    pallas_call x8, Pallas kernels, gram_call(): call(kernel, [((16, SLOT_ROWS[slot], 128), jnp.float32)] * outs, 'v' * le...  6.28 us
    pallas_call x1, Pallas kernels, cast_call(): call(cast_kernel, [((128, 256), f32), ((2, 128, 384), f32), ((4, 128, 640...  2.39 us
  transfers between devices with their start and end apart: 32, of which 16 were waited for; matrix products, arithmetic and copies ran while one was open for 1% of the time, Pallas kernels for 8%

profile of v1, /device:TPU:1, one launch (start us, length us, event | category | flops | bytes accessed | tf_op | source)
XLA Modules:
  0.0 89.5 jit_solution(7301232740334830104)
XLA Ops:
  0.0 2.4 %shard_map.55 = (f32[128,256]{1,0:T(8,128)S(1)}, f32[2,128,384]{2,1,0:T(8,128)S(1)}, f32[4,128,640]{2,1,0:T(8,128)S(1)}, f32[2,128,384]{2,1,0:T(8,128)S(1)}, f32...) custom-call(bf16[128,16384]{1,0:T(8,128)(2,1)} %feat.1), custom_call_target="tpu_custom_call" | custom-call | flops 1000000 | bytes 6291456 | tf_op jit(solution)/shard_map/pallas_call | solution.py:115
  2.4 1.4 %collective-permute-start.6 = (f32[4,128,640]{2,1,0:T(8,128)S(1)}, f32[4,128,640]{2,1,0:T(8,128)S(1)}, u32[]{:S(2)}, u32[]{:S(2)}) collective-permute-start(f32[4,128,640]{2,1,0:T(8,128)S(1)} %get-tuple-element.44), channel_id=1, source_target_pairs={{0,8},{1,9},{2,10},{3,11},{4,12},{5,13},{6,14},{7,15},{8,0},{9,1},... | collective-permute-start | bytes 3932168 | tf_op jit(solution)/shard_map/ppermute | solution.py:405
  3.9 0.4 collective-permute-start.3
  4.5 0.4 collective-permute-start.2
  4.9 5.4 %collective-permute-done.2.other_salt = s32[1,128]{1,0:T(1,128)S(1)} collective-permute-done((s32[1,128]{1,0:T(1,128)S(1)}, s32[1,128]{1,0:T(1,128)S(1)}, u32[]{:S(2)}, u32[]{:S(2)}) %collective-permute-start.2) | collective-permute-done | bytes 544 | tf_op jit(solution)/shard_map/ppermute | solution.py:405
  10.3 0.4 collective-permute-start
  10.6 0.9 shard_map.58
  11.8 0.4 shard_map.59
  12.3 1.4 %collective-permute-start.4 = (f32[16,96,128]{2,1,0:T(8,128)S(1)}, f32[16,96,128]{2,1,0:T(8,128)S(1)}, u32[]{:S(2)}, u32[]{:S(2)}) collective-permute-start(f32[16,96,128]{2,1,0:T(8,128)S(1)} %shard_map.59), channel_id=1, source_target_pairs={{0,3},{1,2},{2,1},{3,0},{4,7},{5,6},{6,5},{7,4},{8,9},{9,8},{10,11... | collective-permute-start | bytes 2359304 | tf_op jit(solution)/shard_map/ppermute | solution.py:405
  13.7 0.9 %shard_map.61 = (f32[16,80,128]{2,1,0:T(8,128)S(1)}, f32[16,80,128]{2,1,0:T(8,128)S(1)}) custom-call(bf16[4,128,640]{2,1,0:T(8,128)(2,1)S(1)} %get-tuple-element.43.own, f32[4,128,640]{2,1,0:T(8,128)S(1)} %collective-permute-done.6.other, bf16[2,256,256]{2,1,0:T(8,128)(2,1)S(1)} %get-tuple-element.39.q, s32[256,128]{1,0:T(8,128)S(1)} %get-tuple-element.40.salt, ...), custom_call_target="tpu_custom_call" | custom-call | flops 128000000 | bytes 3145728 | tf_op jit(solution)/shard_map/pallas_call | solution.py:332
  14.6 3.8 %collective-permute-start.9 = (f32[16,80,128]{2,1,0:T(8,128)S(1)}, f32[16,80,128]{2,1,0:T(8,128)S(1)}, u32[]{:S(2)}, u32[]{:S(2)}) collective-permute-start(f32[16,80,128]{2,1,0:T(8,128)S(1)} %get-tuple-element.49), channel_id=1, source_target_pairs={{0,16},{1,17},{2,18},{3,19},{4,20},{5,21},{6,22},{7,23},{8,56},{9,... | collective-permute-start | bytes 1966088 | tf_op jit(solution)/shard_map/ppermute | solution.py:405
  18.5 0.7 shard_map.60
  19.2 1.4 %collective-permute-start.7 = (f32[16,96,128]{2,1,0:T(8,128)S(1)}, f32[16,96,128]{2,1,0:T(8,128)S(1)}, u32[]{:S(2)}, u32[]{:S(2)}) collective-permute-start(f32[16,96,128]{2,1,0:T(8,128)S(1)} %get-tuple-element.46), channel_id=1, source_target_pairs={{0,68},{1,69},{2,70},{3,71},{4,64},{5,65},{6,66},{7,67},{8,12},{9,... | collective-permute-start | bytes 2359304 | tf_op jit(solution)/shard_map/ppermute | solution.py:405
  20.6 0.6 shard_map.57
  21.2 2.3 %collective-permute-done.4 = f32[16,96,128]{2,1,0:T(8,128)S(1)} collective-permute-done((f32[16,96,128]{2,1,0:T(8,128)S(1)}, f32[16,96,128]{2,1,0:T(8,128)S(1)}, u32[]{:S(2)}, u32[]{:S(2)}) %collective-permute-start.4) | collective-permute-done | bytes 786464 | tf_op jit(solution)/shard_map/ppermute | solution.py:405
  23.6 1.5 %collective-permute-start.5 = (f32[8,96,128]{2,1,0:T(8,128)S(1)}, f32[8,96,128]{2,1,0:T(8,128)S(1)}, u32[]{:S(2)}, u32[]{:S(2)}) collective-permute-start(f32[8,96,128]{2,1,0:T(8,128)S(1)} %get-tuple-element.72), channel_id=1, source_target_pairs={{0,68},{1,69},{2,70},{3,71},{4,64},{5,65},{6,66},{7,67},{8,12},{9,... | collective-permute-start | bytes 1179656 | tf_op jit(solution)/shard_map/ppermute | solution.py:405
  25.1 1.6 %collective-permute-done.9 = f32[16,80,128]{2,1,0:T(8,128)S(1)} collective-permute-done((f32[16,80,128]{2,1,0:T(8,128)S(1)}, f32[16,80,128]{2,1,0:T(8,128)S(1)}, u32[]{:S(2)}, u32[]{:S(2)}) %collective-permute-start.9) | collective-permute-done | bytes 655392 | tf_op jit(solution)/shard_map/ppermute | solution.py:405
  26.8 0.3 collective-permute-start.10
  27.1 1.1 %shard_map.65 = (f32[16,96,128]{2,1,0:T(8,128)S(1)}, f32[16,96,128]{2,1,0:T(8,128)S(1)}) custom-call(bf16[8,128,1024]{2,1,0:T(8,128)(2,1)S(1)} %get-tuple-element.35.mine, f32[4,128,1024]{2,1,0:T(8,128)S(1)} %collective-permute-done.17.other, bf16[2,256,256]{2,1,0:T(8,128)(2,1)S(1)} %get-tuple-element.39.q, s32[256,128]{1,0:T(8,128)S(1)} %get-tuple-element.40.salt, ...), custom_call_target="tpu_custom_call" | custom-call | flops 192000000 | bytes 3145728 | tf_op jit(solution)/shard_map/pallas_call | solution.py:332
  28.2 1.1 %collective-permute-start.20 = (f32[16,96,128]{2,1,0:T(8,128)S(1)}, f32[16,96,128]{2,1,0:T(8,128)S(1)}, u32[]{:S(2)}, u32[]{:S(2)}) collective-permute-start(f32[16,96,128]{2,1,0:T(8,128)S(1)} %get-tuple-element.56), channel_id=1, source_target_pairs={{0,68},{1,69},{2,70},{3,71},{4,64},{5,65},{6,66},{7,67},{8,12},{9,... | collective-permute-start | bytes 2359304 | tf_op jit(solution)/shard_map/ppermute | solution.py:405
  29.3 0.6 shard_map.64
  30.0 1.3 %collective-permute-start.18 = (f32[16,96,128]{2,1,0:T(8,128)S(1)}, f32[16,96,128]{2,1,0:T(8,128)S(1)}, u32[]{:S(2)}, u32[]{:S(2)}) collective-permute-start(f32[16,96,128]{2,1,0:T(8,128)S(1)} %shard_map.64), channel_id=1, source_target_pairs={{0,3},{1,2},{2,1},{3,0},{4,7},{5,6},{6,5},{7,4},{8,9},{9,8},{10,11... | collective-permute-start | bytes 2359304 | tf_op jit(solution)/shard_map/ppermute | solution.py:405
  31.4 2.8 %collective-permute-start.8 = (f32[8,96,128]{2,1,0:T(8,128)S(1)}, f32[8,96,128]{2,1,0:T(8,128)S(1)}, u32[]{:S(2)}, u32[]{:S(2)}) collective-permute-start(f32[8,96,128]{2,1,0:T(8,128)S(1)} %get-tuple-element.70), channel_id=1, source_target_pairs={{0,16},{1,17},{2,18},{3,19},{4,20},{5,21},{6,22},{7,23},{8,56},{9,... | collective-permute-start | bytes 1179656 | tf_op jit(solution)/shard_map/ppermute | solution.py:405
  34.2 0.4 collective-permute-done.5
  34.7 0.6 shard_map.63
  35.4 1.2 %shard_map.66 = (f32[16,80,128]{2,1,0:T(8,128)S(1)}, f32[16,80,128]{2,1,0:T(8,128)S(1)}) custom-call(bf16[8,128,1024]{2,1,0:T(8,128)(2,1)S(1)} %get-tuple-element.35.mine, f32[4,128,1024]{2,1,0:T(8,128)S(1)} %collective-permute-done.17.other, bf16[2,256,256]{2,1,0:T(8,128)(2,1)S(1)} %get-tuple-element.39.q, s32[256,128]{1,0:T(8,128)S(1)} %get-tuple-element.40.salt, ...), custom_call_target="tpu_custom_call" | custom-call | flops 128000000 | bytes 3145728 | tf_op jit(solution)/shard_map/pallas_call | solution.py:332
  36.6 2.7 %collective-permute-start.22 = (f32[16,80,128]{2,1,0:T(8,128)S(1)}, f32[16,80,128]{2,1,0:T(8,128)S(1)}, u32[]{:S(2)}, u32[]{:S(2)}) collective-permute-start(f32[16,80,128]{2,1,0:T(8,128)S(1)} %get-tuple-element.58), channel_id=1, source_target_pairs={{0,16},{1,17},{2,18},{3,19},{4,20},{5,21},{6,22},{7,23},{8,56},{9,... | collective-permute-start | bytes 1966088 | tf_op jit(solution)/shard_map/ppermute | solution.py:405
  39.7 1.1 %collective-permute-start.13 = (f32[4,80,128]{2,1,0:T(8,128)S(1)}, f32[4,80,128]{2,1,0:T(8,128)S(1)}, u32[]{:S(2)}, u32[]{:S(2)}) collective-permute-start(f32[4,80,128]{2,1,0:T(8,128)S(1)} %get-tuple-element.87), channel_id=1, source_target_pairs={{0,68},{1,69},{2,70},{3,71},{4,64},{5,65},{6,66},{7,67},{8,12},{9,... | collective-permute-start | bytes 491528 | tf_op jit(solution)/shard_map/ppermute | solution.py:405
  40.8 2.2 %collective-permute-done.20 = f32[16,96,128]{2,1,0:T(8,128)S(1)} collective-permute-done((f32[16,96,128]{2,1,0:T(8,128)S(1)}, f32[16,96,128]{2,1,0:T(8,128)S(1)}, u32[]{:S(2)}, u32[]{:S(2)}) %collective-permute-start.20) | collective-permute-done | bytes 786464 | tf_op jit(solution)/shard_map/ppermute | solution.py:405
  43.4 0.9 %collective-permute-start.21 = (f32[8,96,128]{2,1,0:T(8,128)S(1)}, f32[8,96,128]{2,1,0:T(8,128)S(1)}, u32[]{:S(2)}, u32[]{:S(2)}) collective-permute-start(f32[8,96,128]{2,1,0:T(8,128)S(1)} %get-tuple-element.66), channel_id=1, source_target_pairs={{0,16},{1,17},{2,18},{3,19},{4,20},{5,21},{6,22},{7,23},{8,56},{9,... | collective-permute-start | bytes 1179656 | tf_op jit(solution)/shard_map/ppermute | solution.py:405
  44.4 4.4 %collective-permute-done.22 = f32[16,80,128]{2,1,0:T(8,128)S(1)} collective-permute-done((f32[16,80,128]{2,1,0:T(8,128)S(1)}, f32[16,80,128]{2,1,0:T(8,128)S(1)}, u32[]{:S(2)}, u32[]{:S(2)}) %collective-permute-start.22) | collective-permute-done | bytes 655392 | tf_op jit(solution)/shard_map/ppermute | solution.py:405
  49.0 3.8 %collective-permute-done.21 = f32[8,96,128]{2,1,0:T(8,128)S(1)} collective-permute-done((f32[8,96,128]{2,1,0:T(8,128)S(1)}, f32[8,96,128]{2,1,0:T(8,128)S(1)}, u32[]{:S(2)}, u32[]{:S(2)}) %collective-permute-start.21) | collective-permute-done | bytes 393248 | tf_op jit(solution)/shard_map/ppermute | solution.py:405
  53.0 2.8 %collective-permute-done.19 = f32[8,96,128]{2,1,0:T(8,128)S(1)} collective-permute-done((f32[8,96,128]{2,1,0:T(8,128)S(1)}, f32[8,96,128]{2,1,0:T(8,128)S(1)}, u32[]{:S(2)}, u32[]{:S(2)}) %collective-permute-start.19) | collective-permute-done | bytes 393248 | tf_op jit(solution)/shard_map/ppermute | solution.py:405
  55.8 3.2 %collective-permute-done.23 = f32[8,80,128]{2,1,0:T(8,128)S(1)} collective-permute-done((f32[8,80,128]{2,1,0:T(8,128)S(1)}, f32[8,80,128]{2,1,0:T(8,128)S(1)}, u32[]{:S(2)}, u32[]{:S(2)}) %collective-permute-start.23) | collective-permute-done | bytes 327712 | tf_op jit(solution)/shard_map/ppermute | solution.py:405
  59.0 2.9 %collective-permute-start.24 = (f32[4,96,128]{2,1,0:T(8,128)S(1)}, f32[4,96,128]{2,1,0:T(8,128)S(1)}, u32[]{:S(2)}, u32[]{:S(2)}) collective-permute-start(f32[4,96,128]{2,1,0:T(8,128)S(1)} %get-tuple-element.79), channel_id=1, source_target_pairs={{0,16},{1,17},{2,18},{3,19},{4,20},{5,21},{6,22},{7,23},{8,56},{9,... | collective-permute-start | bytes 589832 | tf_op jit(solution)/shard_map/ppermute | solution.py:405
  62.3 3.9 %collective-permute-start.15 = (f32[272,128]{1,0:T(8,128)S(1)}, f32[272,128]{1,0:T(8,128)S(1)}, u32[]{:S(2)}, u32[]{:S(2)}) collective-permute-start(f32[272,128]{1,0:T(8,128)S(1)} %get-tuple-element.52), channel_id=1, source_target_pairs={{0,48},{1,49},{2,50},{3,51},{4,52},{5,53},{6,54},{7,55},{8,24},{9,... | collective-permute-start | bytes 417800 | tf_op jit(solution)/shard_map/ppermute | solution.py:405
  66.2 0.3 collective-permute-done.26.refs_5_
  66.5 1.6 %collective-permute-start.16 = (f32[272,128]{1,0:T(8,128)S(1)}, f32[272,128]{1,0:T(8,128)S(1)}, u32[]{:S(2)}, u32[]{:S(2)}) collective-permute-start(f32[272,128]{1,0:T(8,128)S(1)} %get-tuple-element.53), channel_id=1, source_target_pairs={{0,4},{1,5},{2,6},{3,7},{4,0},{5,1},{6,2},{7,3},{8,76},{9,77},{10,... | collective-permute-start | bytes 417800 | tf_op jit(solution)/shard_map/ppermute | solution.py:405
  68.2 2.1 %collective-permute-start.27 = (f32[272,128]{1,0:T(8,128)S(1)}, f32[272,128]{1,0:T(8,128)S(1)}, u32[]{:S(2)}, u32[]{:S(2)}) collective-permute-start(f32[272,128]{1,0:T(8,128)S(1)} %get-tuple-element.59), channel_id=1, source_target_pairs={{0,53},{1,52},{2,55},{3,54},{4,49},{5,48},{6,51},{7,50},{8,95},{9,... | collective-permute-start | bytes 417800 | tf_op jit(solution)/shard_map/ppermute | solution.py:405
  70.3 2.3 %collective-permute-start.28 = (f32[272,128]{1,0:T(8,128)S(1)}, f32[272,128]{1,0:T(8,128)S(1)}, u32[]{:S(2)}, u32[]{:S(2)}) collective-permute-start(f32[272,128]{1,0:T(8,128)S(1)} %get-tuple-element.60), channel_id=1, source_target_pairs={{0,49},{1,48},{2,51},{3,50},{4,53},{5,52},{6,55},{7,54},{8,27},{9,... | collective-permute-start | bytes 417800 | tf_op jit(solution)/shard_map/ppermute | solution.py:405
  72.6 3.1 %collective-permute-start.29 = (f32[272,128]{1,0:T(8,128)S(1)}, f32[272,128]{1,0:T(8,128)S(1)}, u32[]{:S(2)}, u32[]{:S(2)}) collective-permute-start(f32[272,128]{1,0:T(8,128)S(1)} %get-tuple-element.61), channel_id=1, source_target_pairs={{0,5},{1,4},{2,7},{3,6},{4,1},{5,0},{6,3},{7,2},{8,79},{9,78},{10,... | collective-permute-start | bytes 417800 | tf_op jit(solution)/shard_map/ppermute | solution.py:405
  75.7 0.9 %collective-permute-start.30 = (f32[272,128]{1,0:T(8,128)S(1)}, f32[272,128]{1,0:T(8,128)S(1)}, u32[]{:S(2)}, u32[]{:S(2)}) collective-permute-start(f32[272,128]{1,0:T(8,128)S(1)} %get-tuple-element.62), channel_id=1, source_target_pairs={{0,1},{1,0},{2,3},{3,2},{4,5},{5,4},{6,7},{7,6},{8,11},{9,10},{10,... | collective-permute-start | bytes 417800 | tf_op jit(solution)/shard_map/ppermute | solution.py:405
  76.6 1.1 %collective-permute-done.27.refs_4_ = f32[272,128]{1,0:T(8,128)S(1)} collective-permute-done((f32[272,128]{1,0:T(8,128)S(1)}, f32[272,128]{1,0:T(8,128)S(1)}, u32[]{:S(2)}, u32[]{:S(2)}) %collective-permute-start.27) | collective-permute-done | bytes 139296 | tf_op jit(solution)/shard_map/ppermute | solution.py:405
  77.9 2.0 %collective-permute-done.29.refs_6_ = f32[272,128]{1,0:T(8,128)S(1)} collective-permute-done((f32[272,128]{1,0:T(8,128)S(1)}, f32[272,128]{1,0:T(8,128)S(1)}, u32[]{:S(2)}, u32[]{:S(2)}) %collective-permute-start.29) | collective-permute-done | bytes 139296 | tf_op jit(solution)/shard_map/ppermute | solution.py:405
  79.9 0.9 %collective-permute-done.30.refs_7_ = f32[272,128]{1,0:T(8,128)S(1)} collective-permute-done((f32[272,128]{1,0:T(8,128)S(1)}, f32[272,128]{1,0:T(8,128)S(1)}, u32[]{:S(2)}, u32[]{:S(2)}) %collective-permute-start.30) | collective-permute-done | bytes 139296 | tf_op jit(solution)/shard_map/ppermute | solution.py:405
  80.9 6.9 %collective-permute-start.31 = (f32[136,128]{1,0:T(8,128)S(1)}, f32[136,128]{1,0:T(8,128)S(1)}, u32[]{:S(2)}, u32[]{:S(2)}) collective-permute-start(f32[136,128]{1,0:T(8,128)S(1)} %get-tuple-element.64), channel_id=1, source_target_pairs={{0,8},{1,9},{2,10},{3,11},{4,12},{5,13},{6,14},{7,15},{8,0},{9,1},... | collective-permute-start | bytes 208904 | tf_op jit(solution)/shard_map/ppermute | solution.py:405
  87.8 0.9 %collective-permute-done.31.other = f32[136,128]{1,0:T(8,128)S(1)} collective-permute-done((f32[136,128]{1,0:T(8,128)S(1)}, f32[136,128]{1,0:T(8,128)S(1)}, u32[]{:S(2)}, u32[]{:S(2)}) %collective-permute-start.31) | collective-permute-done | bytes 69664 | tf_op jit(solution)/shard_map/ppermute | solution.py:405
  88.7 0.8 shard_map.69
  (51 shorter events, 2.8 us)
Async XLA Ops:
  0.0 4.5 %copy-start.3 = (s32[128]{0:T(128)S(1)}, s32[128]{0:T(128)}, u32[]{:S(2)}) copy-start(s32[128]{0:T(128)} %param.6) | copy-start | bytes 1540
  0.0 10.6 %copy-start = (s32[16384]{0:T(1024)S(1)}, s32[16384]{0:T(1024)}, u32[]{:S(2)}) copy-start(s32[16384]{0:T(1024)} %param.7) | copy-start | bytes 196612
  0.0 10.6 %copy-start.1 = (s32[16384]{0:T(1024)S(1)}, s32[16384]{0:T(1024)}, u32[]{:S(2)}) copy-start(s32[16384]{0:T(1024)} %param.8) | copy-start | bytes 196612
  0.0 10.6 %copy-start.2 = (s32[16384]{0:T(1024)S(1)}, s32[16384]{0:T(1024)}, u32[]{:S(2)}) copy-start(s32[16384]{0:T(1024)} %param.9) | copy-start | bytes 196612
  2.4 11.3 %collective-permute-start.6 = (f32[4,128,640]{2,1,0:T(8,128)S(1)}, f32[4,128,640]{2,1,0:T(8,128)S(1)}, u32[]{:S(2)}, u32[]{:S(2)}) collective-permute-start(f32[4,128,640]{2,1,0:T(8,128)S(1)} %get-tuple-element.44), channel_id=1, source_target_pairs={{0,8},{1,9},{2,10},{3,11},{4,12},{5,13},{6,14},{7,15},{8,0},{9,1},... | collective-permute-start | bytes 3932168 | tf_op jit(solution)/shard_map/ppermute | solution.py:405
  3.9 23.3 %collective-permute-start.17 = (f32[4,128,1024]{2,1,0:T(8,128)S(1)}, f32[4,128,1024]{2,1,0:T(8,128)S(1)}, u32[]{:S(2)}, u32[]{:S(2)}) collective-permute-start(f32[4,128,1024]{2,1,0:T(8,128)S(1)} %get-tuple-element.54), channel_id=1, source_target_pairs={{0,8},{1,9},{2,10},{3,11},{4,12},{5,13},{6,14},{7,15},{8,0},{9,1},... | collective-permute-start | bytes 6291464 | tf_op jit(solution)/shard_map/ppermute | solution.py:405
  3.9 7.9 %collective-permute-start.3 = (f32[2,128,384]{2,1,0:T(8,128)S(1)}, f32[2,128,384]{2,1,0:T(8,128)S(1)}, u32[]{:S(2)}, u32[]{:S(2)}) collective-permute-start(f32[2,128,384]{2,1,0:T(8,128)S(1)} %get-tuple-element.42), channel_id=1, source_target_pairs={{0,8},{1,9},{2,10},{3,11},{4,12},{5,13},{6,14},{7,15},{8,0},{9,1},... | collective-permute-start | bytes 1179656 | tf_op jit(solution)/shard_map/ppermute | solution.py:405
  4.4 7.1 %collective-permute-start.1 = (f32[128,256]{1,0:T(8,128)S(1)}, f32[128,256]{1,0:T(8,128)S(1)}, u32[]{:S(2)}, u32[]{:S(2)}) collective-permute-start(f32[128,256]{1,0:T(8,128)S(1)} %get-tuple-element.38), channel_id=1, source_target_pairs={{0,8},{1,9},{2,10},{3,11},{4,12},{5,13},{6,14},{7,15},{8,0},{9,1},... | collective-permute-start | bytes 393224 | tf_op jit(solution)/shard_map/ppermute | solution.py:405
  4.5 5.8 %collective-permute-start.2 = (s32[1,128]{1,0:T(1,128)S(1)}, s32[1,128]{1,0:T(1,128)S(1)}, u32[]{:S(2)}, u32[]{:S(2)}) collective-permute-start(s32[1,128]{1,0:T(1,128)S(1)} %bitcast.34), channel_id=1, source_target_pairs={{0,8},{1,9},{2,10},{3,11},{4,12},{5,13},{6,14},{7,15},{8,0},{9,1},... | collective-permute-start | bytes 1544 | tf_op jit(solution)/shard_map/ppermute | solution.py:405
  10.3 3.4 %collective-permute-start = (f32[2,128,384]{2,1,0:T(8,128)S(1)}, f32[2,128,384]{2,1,0:T(8,128)S(1)}, u32[]{:S(2)}, u32[]{:S(2)}) collective-permute-start(f32[2,128,384]{2,1,0:T(8,128)S(1)} %get-tuple-element.36), channel_id=1, source_target_pairs={{0,8},{1,9},{2,10},{3,11},{4,12},{5,13},{6,14},{7,15},{8,0},{9,1},... | collective-permute-start | bytes 1179656 | tf_op jit(solution)/shard_map/ppermute | solution.py:405
  12.3 11.2 %collective-permute-start.4 = (f32[16,96,128]{2,1,0:T(8,128)S(1)}, f32[16,96,128]{2,1,0:T(8,128)S(1)}, u32[]{:S(2)}, u32[]{:S(2)}) collective-permute-start(f32[16,96,128]{2,1,0:T(8,128)S(1)} %shard_map.59), channel_id=1, source_target_pairs={{0,3},{1,2},{2,1},{3,0},{4,7},{5,6},{6,5},{7,4},{8,9},{9,8},{10,11... | collective-permute-start | bytes 2359304 | tf_op jit(solution)/shard_map/ppermute | solution.py:405
  14.6 12.1 %collective-permute-start.9 = (f32[16,80,128]{2,1,0:T(8,128)S(1)}, f32[16,80,128]{2,1,0:T(8,128)S(1)}, u32[]{:S(2)}, u32[]{:S(2)}) collective-permute-start(f32[16,80,128]{2,1,0:T(8,128)S(1)} %get-tuple-element.49), channel_id=1, source_target_pairs={{0,16},{1,17},{2,18},{3,19},{4,20},{5,21},{6,22},{7,23},{8,56},{9,... | collective-permute-start | bytes 1966088 | tf_op jit(solution)/shard_map/ppermute | solution.py:405
  19.2 12.1 %collective-permute-start.7 = (f32[16,96,128]{2,1,0:T(8,128)S(1)}, f32[16,96,128]{2,1,0:T(8,128)S(1)}, u32[]{:S(2)}, u32[]{:S(2)}) collective-permute-start(f32[16,96,128]{2,1,0:T(8,128)S(1)} %get-tuple-element.46), channel_id=1, source_target_pairs={{0,68},{1,69},{2,70},{3,71},{4,64},{5,65},{6,66},{7,67},{8,12},{9,... | collective-permute-start | bytes 2359304 | tf_op jit(solution)/shard_map/ppermute | solution.py:405
  23.6 11.0 %collective-permute-start.5 = (f32[8,96,128]{2,1,0:T(8,128)S(1)}, f32[8,96,128]{2,1,0:T(8,128)S(1)}, u32[]{:S(2)}, u32[]{:S(2)}) collective-permute-start(f32[8,96,128]{2,1,0:T(8,128)S(1)} %get-tuple-element.72), channel_id=1, source_target_pairs={{0,68},{1,69},{2,70},{3,71},{4,64},{5,65},{6,66},{7,67},{8,12},{9,... | collective-permute-start | bytes 1179656 | tf_op jit(solution)/shard_map/ppermute | solution.py:405
  26.8 9.8 %collective-permute-start.10 = (f32[8,80,128]{2,1,0:T(8,128)S(1)}, f32[8,80,128]{2,1,0:T(8,128)S(1)}, u32[]{:S(2)}, u32[]{:S(2)}) collective-permute-start(f32[8,80,128]{2,1,0:T(8,128)S(1)} %get-tuple-element.76), channel_id=1, source_target_pairs={{0,3},{1,2},{2,1},{3,0},{4,7},{5,6},{6,5},{7,4},{8,9},{9,8},{10,11... | collective-permute-start | bytes 983048 | tf_op jit(solution)/shard_map/ppermute | solution.py:405
  28.2 14.8 %collective-permute-start.20 = (f32[16,96,128]{2,1,0:T(8,128)S(1)}, f32[16,96,128]{2,1,0:T(8,128)S(1)}, u32[]{:S(2)}, u32[]{:S(2)}) collective-permute-start(f32[16,96,128]{2,1,0:T(8,128)S(1)} %get-tuple-element.56), channel_id=1, source_target_pairs={{0,68},{1,69},{2,70},{3,71},{4,64},{5,65},{6,66},{7,67},{8,12},{9,... | collective-permute-start | bytes 2359304 | tf_op jit(solution)/shard_map/ppermute | solution.py:405
  30.0 13.4 %collective-permute-start.18 = (f32[16,96,128]{2,1,0:T(8,128)S(1)}, f32[16,96,128]{2,1,0:T(8,128)S(1)}, u32[]{:S(2)}, u32[]{:S(2)}) collective-permute-start(f32[16,96,128]{2,1,0:T(8,128)S(1)} %shard_map.64), channel_id=1, source_target_pairs={{0,3},{1,2},{2,1},{3,0},{4,7},{5,6},{6,5},{7,4},{8,9},{9,8},{10,11... | collective-permute-start | bytes 2359304 | tf_op jit(solution)/shard_map/ppermute | solution.py:405
  31.4 8.3 %collective-permute-start.8 = (f32[8,96,128]{2,1,0:T(8,128)S(1)}, f32[8,96,128]{2,1,0:T(8,128)S(1)}, u32[]{:S(2)}, u32[]{:S(2)}) collective-permute-start(f32[8,96,128]{2,1,0:T(8,128)S(1)} %get-tuple-element.70), channel_id=1, source_target_pairs={{0,16},{1,17},{2,18},{3,19},{4,20},{5,21},{6,22},{7,23},{8,56},{9,... | collective-permute-start | bytes 1179656 | tf_op jit(solution)/shard_map/ppermute | solution.py:405
  34.7 27.3 %collective-permute-start.11 = (f32[4,96,128]{2,1,0:T(8,128)S(1)}, f32[4,96,128]{2,1,0:T(8,128)S(1)}, u32[]{:S(2)}, u32[]{:S(2)}) collective-permute-start(f32[4,96,128]{2,1,0:T(8,128)S(1)} %get-tuple-element.83), channel_id=1, source_target_pairs={{0,16},{1,17},{2,18},{3,19},{4,20},{5,21},{6,22},{7,23},{8,56},{9,... | collective-permute-start | bytes 589832 | tf_op jit(solution)/shard_map/ppermute | solution.py:405
  36.6 12.2 %collective-permute-start.22 = (f32[16,80,128]{2,1,0:T(8,128)S(1)}, f32[16,80,128]{2,1,0:T(8,128)S(1)}, u32[]{:S(2)}, u32[]{:S(2)}) collective-permute-start(f32[16,80,128]{2,1,0:T(8,128)S(1)} %get-tuple-element.58), channel_id=1, source_target_pairs={{0,16},{1,17},{2,18},{3,19},{4,20},{5,21},{6,22},{7,23},{8,56},{9,... | collective-permute-start | bytes 1966088 | tf_op jit(solution)/shard_map/ppermute | solution.py:405
  39.7 22.5 %collective-permute-start.13 = (f32[4,80,128]{2,1,0:T(8,128)S(1)}, f32[4,80,128]{2,1,0:T(8,128)S(1)}, u32[]{:S(2)}, u32[]{:S(2)}) collective-permute-start(f32[4,80,128]{2,1,0:T(8,128)S(1)} %get-tuple-element.87), channel_id=1, source_target_pairs={{0,68},{1,69},{2,70},{3,71},{4,64},{5,65},{6,66},{7,67},{8,12},{9,... | collective-permute-start | bytes 491528 | tf_op jit(solution)/shard_map/ppermute | solution.py:405
  43.0 19.1 %collective-permute-start.12 = (f32[4,96,128]{2,1,0:T(8,128)S(1)}, f32[4,96,128]{2,1,0:T(8,128)S(1)}, u32[]{:S(2)}, u32[]{:S(2)}) collective-permute-start(f32[4,96,128]{2,1,0:T(8,128)S(1)} %get-tuple-element.81), channel_id=1, source_target_pairs={{0,3},{1,2},{2,1},{3,0},{4,7},{5,6},{6,5},{7,4},{8,9},{9,8},{10,11... | collective-permute-start | bytes 589832 | tf_op jit(solution)/shard_map/ppermute | solution.py:405
  43.4 9.4 %collective-permute-start.21 = (f32[8,96,128]{2,1,0:T(8,128)S(1)}, f32[8,96,128]{2,1,0:T(8,128)S(1)}, u32[]{:S(2)}, u32[]{:S(2)}) collective-permute-start(f32[8,96,128]{2,1,0:T(8,128)S(1)} %get-tuple-element.66), channel_id=1, source_target_pairs={{0,16},{1,17},{2,18},{3,19},{4,20},{5,21},{6,22},{7,23},{8,56},{9,... | collective-permute-start | bytes 1179656 | tf_op jit(solution)/shard_map/ppermute | solution.py:405
  48.8 6.9 %collective-permute-start.19 = (f32[8,96,128]{2,1,0:T(8,128)S(1)}, f32[8,96,128]{2,1,0:T(8,128)S(1)}, u32[]{:S(2)}, u32[]{:S(2)}) collective-permute-start(f32[8,96,128]{2,1,0:T(8,128)S(1)} %get-tuple-element.68), channel_id=1, source_target_pairs={{0,68},{1,69},{2,70},{3,71},{4,64},{5,65},{6,66},{7,67},{8,12},{9,... | collective-permute-start | bytes 1179656 | tf_op jit(solution)/shard_map/ppermute | solution.py:405
  52.8 6.2 %collective-permute-start.23 = (f32[8,80,128]{2,1,0:T(8,128)S(1)}, f32[8,80,128]{2,1,0:T(8,128)S(1)}, u32[]{:S(2)}, u32[]{:S(2)}) collective-permute-start(f32[8,80,128]{2,1,0:T(8,128)S(1)} %get-tuple-element.74), channel_id=1, source_target_pairs={{0,3},{1,2},{2,1},{3,0},{4,7},{5,6},{6,5},{7,4},{8,9},{9,8},{10,11... | collective-permute-start | bytes 983048 | tf_op jit(solution)/shard_map/ppermute | solution.py:405
  55.7 12.4 %collective-permute-start.25 = (f32[4,96,128]{2,1,0:T(8,128)S(1)}, f32[4,96,128]{2,1,0:T(8,128)S(1)}, u32[]{:S(2)}, u32[]{:S(2)}) collective-permute-start(f32[4,96,128]{2,1,0:T(8,128)S(1)} %get-tuple-element.77), channel_id=1, source_target_pairs={{0,3},{1,2},{2,1},{3,0},{4,7},{5,6},{6,5},{7,4},{8,9},{9,8},{10,11... | collective-permute-start | bytes 589832 | tf_op jit(solution)/shard_map/ppermute | solution.py:405
  59.0 9.1 %collective-permute-start.24 = (f32[4,96,128]{2,1,0:T(8,128)S(1)}, f32[4,96,128]{2,1,0:T(8,128)S(1)}, u32[]{:S(2)}, u32[]{:S(2)}) collective-permute-start(f32[4,96,128]{2,1,0:T(8,128)S(1)} %get-tuple-element.79), channel_id=1, source_target_pairs={{0,16},{1,17},{2,18},{3,19},{4,20},{5,21},{6,22},{7,23},{8,56},{9,... | collective-permute-start | bytes 589832 | tf_op jit(solution)/shard_map/ppermute | solution.py:405
  62.0 4.5 %collective-permute-start.26 = (f32[4,80,128]{2,1,0:T(8,128)S(1)}, f32[4,80,128]{2,1,0:T(8,128)S(1)}, u32[]{:S(2)}, u32[]{:S(2)}) collective-permute-start(f32[4,80,128]{2,1,0:T(8,128)S(1)} %get-tuple-element.85), channel_id=1, source_target_pairs={{0,68},{1,69},{2,70},{3,71},{4,64},{5,65},{6,66},{7,67},{8,12},{9,... | collective-permute-start | bytes 491528 | tf_op jit(solution)/shard_map/ppermute | solution.py:405
  62.2 10.4 %collective-permute-start.14 = (f32[272,128]{1,0:T(8,128)S(1)}, f32[272,128]{1,0:T(8,128)S(1)}, u32[]{:S(2)}, u32[]{:S(2)}) collective-permute-start(f32[272,128]{1,0:T(8,128)S(1)} %get-tuple-element.51), channel_id=1, source_target_pairs={{0,52},{1,53},{2,54},{3,55},{4,48},{5,49},{6,50},{7,51},{8,92},{9,... | collective-permute-start | bytes 417800 | tf_op jit(solution)/shard_map/ppermute | solution.py:405
  62.3 13.4 %collective-permute-start.15 = (f32[272,128]{1,0:T(8,128)S(1)}, f32[272,128]{1,0:T(8,128)S(1)}, u32[]{:S(2)}, u32[]{:S(2)}) collective-permute-start(f32[272,128]{1,0:T(8,128)S(1)} %get-tuple-element.52), channel_id=1, source_target_pairs={{0,48},{1,49},{2,50},{3,51},{4,52},{5,53},{6,54},{7,55},{8,24},{9,... | collective-permute-start | bytes 417800 | tf_op jit(solution)/shard_map/ppermute | solution.py:405
  66.5 10.1 %collective-permute-start.16 = (f32[272,128]{1,0:T(8,128)S(1)}, f32[272,128]{1,0:T(8,128)S(1)}, u32[]{:S(2)}, u32[]{:S(2)}) collective-permute-start(f32[272,128]{1,0:T(8,128)S(1)} %get-tuple-element.53), channel_id=1, source_target_pairs={{0,4},{1,5},{2,6},{3,7},{4,0},{5,1},{6,2},{7,3},{8,76},{9,77},{10,... | collective-permute-start | bytes 417800 | tf_op jit(solution)/shard_map/ppermute | solution.py:405
  68.2 9.5 %collective-permute-start.27 = (f32[272,128]{1,0:T(8,128)S(1)}, f32[272,128]{1,0:T(8,128)S(1)}, u32[]{:S(2)}, u32[]{:S(2)}) collective-permute-start(f32[272,128]{1,0:T(8,128)S(1)} %get-tuple-element.59), channel_id=1, source_target_pairs={{0,53},{1,52},{2,55},{3,54},{4,49},{5,48},{6,51},{7,50},{8,95},{9,... | collective-permute-start | bytes 417800 | tf_op jit(solution)/shard_map/ppermute | solution.py:405
  70.3 7.6 %collective-permute-start.28 = (f32[272,128]{1,0:T(8,128)S(1)}, f32[272,128]{1,0:T(8,128)S(1)}, u32[]{:S(2)}, u32[]{:S(2)}) collective-permute-start(f32[272,128]{1,0:T(8,128)S(1)} %get-tuple-element.60), channel_id=1, source_target_pairs={{0,49},{1,48},{2,51},{3,50},{4,53},{5,52},{6,55},{7,54},{8,27},{9,... | collective-permute-start | bytes 417800 | tf_op jit(solution)/shard_map/ppermute | solution.py:405
  72.6 7.2 %collective-permute-start.29 = (f32[272,128]{1,0:T(8,128)S(1)}, f32[272,128]{1,0:T(8,128)S(1)}, u32[]{:S(2)}, u32[]{:S(2)}) collective-permute-start(f32[272,128]{1,0:T(8,128)S(1)} %get-tuple-element.61), channel_id=1, source_target_pairs={{0,5},{1,4},{2,7},{3,6},{4,1},{5,0},{6,3},{7,2},{8,79},{9,78},{10,... | collective-permute-start | bytes 417800 | tf_op jit(solution)/shard_map/ppermute | solution.py:405
  75.7 5.1 %collective-permute-start.30 = (f32[272,128]{1,0:T(8,128)S(1)}, f32[272,128]{1,0:T(8,128)S(1)}, u32[]{:S(2)}, u32[]{:S(2)}) collective-permute-start(f32[272,128]{1,0:T(8,128)S(1)} %get-tuple-element.62), channel_id=1, source_target_pairs={{0,1},{1,0},{2,3},{3,2},{4,5},{5,4},{6,7},{7,6},{8,11},{9,10},{10,... | collective-permute-start | bytes 417800 | tf_op jit(solution)/shard_map/ppermute | solution.py:405
  80.9 7.8 %collective-permute-start.31 = (f32[136,128]{1,0:T(8,128)S(1)}, f32[136,128]{1,0:T(8,128)S(1)}, u32[]{:S(2)}, u32[]{:S(2)}) collective-permute-start(f32[136,128]{1,0:T(8,128)S(1)} %get-tuple-element.64), channel_id=1, source_target_pairs={{0,8},{1,9},{2,10},{3,11},{4,12},{5,13},{6,14},{7,15},{8,0},{9,1},... | collective-permute-start | bytes 208904 | tf_op jit(solution)/shard_map/ppermute | solution.py:405

commit v2 on v1

--- a/solution.py
+++ b/solution.py
@@ -82,7 +82,7 @@
     )
 
 
-ORDER = [(xa, c, xb) for xb in (0, 1) for xa in (1, 0) for c in (0, 1)]
+ORDER = [(xa, c, xb) for xb in (1, 0) for xa in (1, 0) for c in (0, 1)]
 
 
 def cast_kernel(feat, outq, out0s, outa, out0k, outb, mine, queries, block, sems):
@@ -454,7 +454,7 @@
         gots = [third[half, slot] for slot in range(3)]
         joined = join_call(keeps, gots)
         for at in range(4):
-            chunks[half + 2 * (at & 1) + 4 * (at >> 1)] = joined[at]
+            chunks[1 - half + 2 * (at & 1) + 4 * (at >> 1)] = joined[at]
     parts = [chunks[0]]
     for j in LAST:
         parts.append(permute(chunks[j], moves(none, [j & 1, j >> 1 & 1, j >> 2])))
@@ -462,7 +462,7 @@
     return finish_call(keep, permute(send, partner))
 
 
-LAST = (6, 4, 2, 7, 5, 3, 1)
+LAST = (7, 5, 3, 1, 6, 4, 2)
 TURNS = [(half, slot) for half in (0, 1) for slot in range(3)]
 
 

time: 89.6 us -> 92.6 us (1.033)
  starting transfers between devices: 45.8 us -> 53 us
  waiting for transfers between devices: 31.8 us -> 27.7 us
    ppermute x32, starting transfers between devices: 45.8 us -> 53 us  [permute(): return lax.ppermute(x, AXES, pairs)]
    ppermute x32, waiting for transfers between devices: 31.8 us -> 27.7 us  [permute(): return lax.ppermute(x, AXES, pairs)]
  transfers between devices with their start and end apart: 32 -> 32, of which waited for: 16 -> 14; matrix products, arithmetic and copies ran while one was open for 1% -> 1% of each run, Pallas kernels for 8% -> 8%
where the time goes in v2:
time: 92.6 us; the launch traced here: 92.5 us
  starting transfers between devices  53 us (57%)
  waiting for transfers between devices  27.7 us (30%)
  Pallas kernels  10.8 us (12%)
    ppermute x32, starting transfers between devices, permute(): return lax.ppermute(x, AXES, pairs)  53 us
    ppermute x32, waiting for transfers between devices, permute(): return lax.ppermute(x, AXES, pairs)  27.7 us
    pallas_call x8, Pallas kernels, gram_call(): call(kernel, [((16, SLOT_ROWS[slot], 128), jnp.float32)] * outs, 'v' * le...  6.26 us
    pallas_call x1, Pallas kernels, cast_call(): call(cast_kernel, [((128, 256), f32), ((2, 128, 384), f32), ((4, 128, 640...  2.38 us
  transfers between devices with their start and end apart: 32, of which 14 were waited for; matrix products, arithmetic and copies ran while one was open for 1% of the time, Pallas kernels for 8%

profile of v2, /device:TPU:1, one launch (start us, length us, event | category | flops | bytes accessed | tf_op | source)
XLA Modules:
  0.0 92.5 jit_solution(18406505347022746301)
XLA Ops:
  0.0 2.4 %shard_map.55 = (f32[128,256]{1,0:T(8,128)S(1)}, f32[2,128,384]{2,1,0:T(8,128)S(1)}, f32[4,128,640]{2,1,0:T(8,128)S(1)}, f32[2,128,384]{2,1,0:T(8,128)S(1)}, f32...) custom-call(bf16[128,16384]{1,0:T(8,128)(2,1)} %feat.1), custom_call_target="tpu_custom_call" | custom-call | flops 1000000 | bytes 6291456 | tf_op jit(solution)/shard_map/pallas_call | solution.py:115
  2.4 1.4 %collective-permute-start.16 = (f32[4,128,640]{2,1,0:T(8,128)S(1)}, f32[4,128,640]{2,1,0:T(8,128)S(1)}, u32[]{:S(2)}, u32[]{:S(2)}) collective-permute-start(f32[4,128,640]{2,1,0:T(8,128)S(1)} %get-tuple-element.51), channel_id=1, source_target_pairs={{0,8},{1,9},{2,10},{3,11},{4,12},{5,13},{6,14},{7,15},{8,0},{9,1},... | collective-permute-start | bytes 3932168 | tf_op jit(solution)/shard_map/ppermute | solution.py:405
  3.9 0.4 collective-permute-start.13
  4.5 0.4 collective-permute-start.2
  4.9 5.4 %collective-permute-done.2.other_salt = s32[1,128]{1,0:T(1,128)S(1)} collective-permute-done((s32[1,128]{1,0:T(1,128)S(1)}, s32[1,128]{1,0:T(1,128)S(1)}, u32[]{:S(2)}, u32[]{:S(2)}) %collective-permute-start.2) | collective-permute-done | bytes 544 | tf_op jit(solution)/shard_map/ppermute | solution.py:405
  10.6 0.9 shard_map.63
  11.8 0.4 shard_map.64
  12.3 1.4 %collective-permute-start.14 = (f32[16,96,128]{2,1,0:T(8,128)S(1)}, f32[16,96,128]{2,1,0:T(8,128)S(1)}, u32[]{:S(2)}, u32[]{:S(2)}) collective-permute-start(f32[16,96,128]{2,1,0:T(8,128)S(1)} %shard_map.64), channel_id=1, source_target_pairs={{0,3},{1,2},{2,1},{3,0},{4,7},{5,6},{6,5},{7,4},{8,9},{9,8},{10,11... | collective-permute-start | bytes 2359304 | tf_op jit(solution)/shard_map/ppermute | solution.py:405
  13.7 0.9 shard_map.66
  14.6 3.8 %collective-permute-start.19 = (f32[16,80,128]{2,1,0:T(8,128)S(1)}, f32[16,80,128]{2,1,0:T(8,128)S(1)}, u32[]{:S(2)}, u32[]{:S(2)}) collective-permute-start(f32[16,80,128]{2,1,0:T(8,128)S(1)} %get-tuple-element.55), channel_id=1, source_target_pairs={{0,16},{1,17},{2,18},{3,19},{4,20},{5,21},{6,22},{7,23},{8,56},{9,... | collective-permute-start | bytes 1966088 | tf_op jit(solution)/shard_map/ppermute | solution.py:405
  18.5 0.7 shard_map.65
  19.2 1.4 %collective-permute-start.17 = (f32[16,96,128]{2,1,0:T(8,128)S(1)}, f32[16,96,128]{2,1,0:T(8,128)S(1)}, u32[]{:S(2)}, u32[]{:S(2)}) collective-permute-start(f32[16,96,128]{2,1,0:T(8,128)S(1)} %get-tuple-element.53), channel_id=1, source_target_pairs={{0,68},{1,69},{2,70},{3,71},{4,64},{5,65},{6,66},{7,67},{8,12},{9,... | collective-permute-start | bytes 2359304 | tf_op jit(solution)/shard_map/ppermute | solution.py:405
  20.5 0.6 shard_map.62
  21.2 2.3 %collective-permute-done.14 = f32[16,96,128]{2,1,0:T(8,128)S(1)} collective-permute-done((f32[16,96,128]{2,1,0:T(8,128)S(1)}, f32[16,96,128]{2,1,0:T(8,128)S(1)}, u32[]{:S(2)}, u32[]{:S(2)}) %collective-permute-start.14) | collective-permute-done | bytes 786464 | tf_op jit(solution)/shard_map/ppermute | solution.py:405
  23.6 1.5 %collective-permute-start.15 = (f32[8,96,128]{2,1,0:T(8,128)S(1)}, f32[8,96,128]{2,1,0:T(8,128)S(1)}, u32[]{:S(2)}, u32[]{:S(2)}) collective-permute-start(f32[8,96,128]{2,1,0:T(8,128)S(1)} %get-tuple-element.68), channel_id=1, source_target_pairs={{0,68},{1,69},{2,70},{3,71},{4,64},{5,65},{6,66},{7,67},{8,12},{9,... | collective-permute-start | bytes 1179656 | tf_op jit(solution)/shard_map/ppermute | solution.py:405
  25.1 1.6 %collective-permute-done.19 = f32[16,80,128]{2,1,0:T(8,128)S(1)} collective-permute-done((f32[16,80,128]{2,1,0:T(8,128)S(1)}, f32[16,80,128]{2,1,0:T(8,128)S(1)}, u32[]{:S(2)}, u32[]{:S(2)}) %collective-permute-start.19) | collective-permute-done | bytes 655392 | tf_op jit(solution)/shard_map/ppermute | solution.py:405
  27.1 0.6 shard_map.58
  27.8 1.3 %collective-permute-start.3 = (f32[16,96,128]{2,1,0:T(8,128)S(1)}, f32[16,96,128]{2,1,0:T(8,128)S(1)}, u32[]{:S(2)}, u32[]{:S(2)}) collective-permute-start(f32[16,96,128]{2,1,0:T(8,128)S(1)} %shard_map.58), channel_id=1, source_target_pairs={{0,3},{1,2},{2,1},{3,0},{4,7},{5,6},{6,5},{7,4},{8,9},{9,8},{10,11... | collective-permute-start | bytes 2359304 | tf_op jit(solution)/shard_map/ppermute | solution.py:405
  29.1 1.1 %shard_map.59 = (f32[16,96,128]{2,1,0:T(8,128)S(1)}, f32[16,96,128]{2,1,0:T(8,128)S(1)}) custom-call(bf16[8,128,1024]{2,1,0:T(8,128)(2,1)S(1)} %get-tuple-element.35.mine, f32[4,128,1024]{2,1,0:T(8,128)S(1)} %collective-permute-done.other, bf16[2,256,256]{2,1,0:T(8,128)(2,1)S(1)} %get-tuple-element.39.q, s32[256,128]{1,0:T(8,128)S(1)} %get-tuple-element.40.salt, ...), custom_call_target="tpu_custom_call" | custom-call | flops 192000000 | bytes 3145728 | tf_op jit(solution)/shard_map/pallas_call | solution.py:332
  30.2 1.1 %collective-permute-start.5 = (f32[16,96,128]{2,1,0:T(8,128)S(1)}, f32[16,96,128]{2,1,0:T(8,128)S(1)}, u32[]{:S(2)}, u32[]{:S(2)}) collective-permute-start(f32[16,96,128]{2,1,0:T(8,128)S(1)} %get-tuple-element.42), channel_id=1, source_target_pairs={{0,68},{1,69},{2,70},{3,71},{4,64},{5,65},{6,66},{7,67},{8,12},{9,... | collective-permute-start | bytes 2359304 | tf_op jit(solution)/shard_map/ppermute | solution.py:405
  31.4 2.8 %collective-permute-start.18 = (f32[8,96,128]{2,1,0:T(8,128)S(1)}, f32[8,96,128]{2,1,0:T(8,128)S(1)}, u32[]{:S(2)}, u32[]{:S(2)}) collective-permute-start(f32[8,96,128]{2,1,0:T(8,128)S(1)} %get-tuple-element.66), channel_id=1, source_target_pairs={{0,16},{1,17},{2,18},{3,19},{4,20},{5,21},{6,22},{7,23},{8,56},{9,... | collective-permute-start | bytes 1179656 | tf_op jit(solution)/shard_map/ppermute | solution.py:405
  34.2 0.4 collective-permute-done.15
  34.7 0.6 shard_map.57
  35.4 1.2 %shard_map.60 = (f32[16,80,128]{2,1,0:T(8,128)S(1)}, f32[16,80,128]{2,1,0:T(8,128)S(1)}) custom-call(bf16[8,128,1024]{2,1,0:T(8,128)(2,1)S(1)} %get-tuple-element.35.mine, f32[4,128,1024]{2,1,0:T(8,128)S(1)} %collective-permute-done.other, bf16[2,256,256]{2,1,0:T(8,128)(2,1)S(1)} %get-tuple-element.39.q, s32[256,128]{1,0:T(8,128)S(1)} %get-tuple-element.40.salt, ...), custom_call_target="tpu_custom_call" | custom-call | flops 128000000 | bytes 3145728 | tf_op jit(solution)/shard_map/pallas_call | solution.py:332
  36.6 2.7 %collective-permute-start.7 = (f32[16,80,128]{2,1,0:T(8,128)S(1)}, f32[16,80,128]{2,1,0:T(8,128)S(1)}, u32[]{:S(2)}, u32[]{:S(2)}) collective-permute-start(f32[16,80,128]{2,1,0:T(8,128)S(1)} %get-tuple-element.45), channel_id=1, source_target_pairs={{0,16},{1,17},{2,18},{3,19},{4,20},{5,21},{6,22},{7,23},{8,56},{9,... | collective-permute-start | bytes 1966088 | tf_op jit(solution)/shard_map/ppermute | solution.py:405
  39.7 1.1 %collective-permute-start.23 = (f32[4,80,128]{2,1,0:T(8,128)S(1)}, f32[4,80,128]{2,1,0:T(8,128)S(1)}, u32[]{:S(2)}, u32[]{:S(2)}) collective-permute-start(f32[4,80,128]{2,1,0:T(8,128)S(1)} %get-tuple-element.85), channel_id=1, source_target_pairs={{0,68},{1,69},{2,70},{3,71},{4,64},{5,65},{6,66},{7,67},{8,12},{9,... | collective-permute-start | bytes 491528 | tf_op jit(solution)/shard_map/ppermute | solution.py:405
  40.8 0.7 collective-permute-done.3
  41.9 1.1 %collective-permute-done.5 = f32[16,96,128]{2,1,0:T(8,128)S(1)} collective-permute-done((f32[16,96,128]{2,1,0:T(8,128)S(1)}, f32[16,96,128]{2,1,0:T(8,128)S(1)}, u32[]{:S(2)}, u32[]{:S(2)}) %collective-permute-start.5) | collective-permute-done | bytes 786464 | tf_op jit(solution)/shard_map/ppermute | solution.py:405
  43.0 1.3 %collective-permute-start.4 = (f32[8,96,128]{2,1,0:T(8,128)S(1)}, f32[8,96,128]{2,1,0:T(8,128)S(1)}, u32[]{:S(2)}, u32[]{:S(2)}) collective-permute-start(f32[8,96,128]{2,1,0:T(8,128)S(1)} %get-tuple-element.72), channel_id=1, source_target_pairs={{0,68},{1,69},{2,70},{3,71},{4,64},{5,65},{6,66},{7,67},{8,12},{9,... | collective-permute-start | bytes 1179656 | tf_op jit(solution)/shard_map/ppermute | solution.py:405
  44.4 4.4 %collective-permute-done.7 = f32[16,80,128]{2,1,0:T(8,128)S(1)} collective-permute-done((f32[16,80,128]{2,1,0:T(8,128)S(1)}, f32[16,80,128]{2,1,0:T(8,128)S(1)}, u32[]{:S(2)}, u32[]{:S(2)}) %collective-permute-start.7) | collective-permute-done | bytes 655392 | tf_op jit(solution)/shard_map/ppermute | solution.py:405
  48.8 2.7 %collective-permute-start.6 = (f32[8,96,128]{2,1,0:T(8,128)S(1)}, f32[8,96,128]{2,1,0:T(8,128)S(1)}, u32[]{:S(2)}, u32[]{:S(2)}) collective-permute-start(f32[8,96,128]{2,1,0:T(8,128)S(1)} %get-tuple-element.70), channel_id=1, source_target_pairs={{0,16},{1,17},{2,18},{3,19},{4,20},{5,21},{6,22},{7,23},{8,56},{9,... | collective-permute-start | bytes 1179656 | tf_op jit(solution)/shard_map/ppermute | solution.py:405
  51.9 5.0 %collective-permute-done.6 = f32[8,96,128]{2,1,0:T(8,128)S(1)} collective-permute-done((f32[8,96,128]{2,1,0:T(8,128)S(1)}, f32[8,96,128]{2,1,0:T(8,128)S(1)}, u32[]{:S(2)}, u32[]{:S(2)}) %collective-permute-start.6) | collective-permute-done | bytes 393248 | tf_op jit(solution)/shard_map/ppermute | solution.py:405
  56.9 2.7 %collective-permute-start.9 = (f32[4,96,128]{2,1,0:T(8,128)S(1)}, f32[4,96,128]{2,1,0:T(8,128)S(1)}, u32[]{:S(2)}, u32[]{:S(2)}) collective-permute-start(f32[4,96,128]{2,1,0:T(8,128)S(1)} %get-tuple-element.83), channel_id=1, source_target_pairs={{0,16},{1,17},{2,18},{3,19},{4,20},{5,21},{6,22},{7,23},{8,56},{9,... | collective-permute-start | bytes 589832 | tf_op jit(solution)/shard_map/ppermute | solution.py:405
  59.8 0.6 collective-permute-start.11
  60.4 1.0 %collective-permute-start.24 = (f32[272,128]{1,0:T(8,128)S(1)}, f32[272,128]{1,0:T(8,128)S(1)}, u32[]{:S(2)}, u32[]{:S(2)}) collective-permute-start(f32[272,128]{1,0:T(8,128)S(1)} %get-tuple-element.56), channel_id=1, source_target_pairs={{0,53},{1,52},{2,55},{3,54},{4,49},{5,48},{6,51},{7,50},{8,95},{9,... | collective-permute-start | bytes 417800 | tf_op jit(solution)/shard_map/ppermute | solution.py:405
  61.4 4.7 %collective-permute-start.25 = (f32[272,128]{1,0:T(8,128)S(1)}, f32[272,128]{1,0:T(8,128)S(1)}, u32[]{:S(2)}, u32[]{:S(2)}) collective-permute-start(f32[272,128]{1,0:T(8,128)S(1)} %get-tuple-element.57), channel_id=1, source_target_pairs={{0,49},{1,48},{2,51},{3,50},{4,53},{5,52},{6,55},{7,54},{8,27},{9,... | collective-permute-start | bytes 417800 | tf_op jit(solution)/shard_map/ppermute | solution.py:405
  66.1 2.1 %collective-permute-start.26 = (f32[272,128]{1,0:T(8,128)S(1)}, f32[272,128]{1,0:T(8,128)S(1)}, u32[]{:S(2)}, u32[]{:S(2)}) collective-permute-start(f32[272,128]{1,0:T(8,128)S(1)} %get-tuple-element.58), channel_id=1, source_target_pairs={{0,5},{1,4},{2,7},{3,6},{4,1},{5,0},{6,3},{7,2},{8,79},{9,78},{10,... | collective-permute-start | bytes 417800 | tf_op jit(solution)/shard_map/ppermute | solution.py:405
  68.3 0.7 collective-permute-start.27
  69.0 2.1 %collective-permute-start.28 = (f32[272,128]{1,0:T(8,128)S(1)}, f32[272,128]{1,0:T(8,128)S(1)}, u32[]{:S(2)}, u32[]{:S(2)}) collective-permute-start(f32[272,128]{1,0:T(8,128)S(1)} %get-tuple-element.60), channel_id=1, source_target_pairs={{0,52},{1,53},{2,54},{3,55},{4,48},{5,49},{6,50},{7,51},{8,92},{9,... | collective-permute-start | bytes 417800 | tf_op jit(solution)/shard_map/ppermute | solution.py:405
  71.1 1.4 %collective-permute-start.29 = (f32[272,128]{1,0:T(8,128)S(1)}, f32[272,128]{1,0:T(8,128)S(1)}, u32[]{:S(2)}, u32[]{:S(2)}) collective-permute-start(f32[272,128]{1,0:T(8,128)S(1)} %get-tuple-element.61), channel_id=1, source_target_pairs={{0,48},{1,49},{2,50},{3,51},{4,52},{5,53},{6,54},{7,55},{8,24},{9,... | collective-permute-start | bytes 417800 | tf_op jit(solution)/shard_map/ppermute | solution.py:405
  72.5 0.4 collective-permute-start.30
  72.9 1.5 %collective-permute-done.26.refs_3_ = f32[272,128]{1,0:T(8,128)S(1)} collective-permute-done((f32[272,128]{1,0:T(8,128)S(1)}, f32[272,128]{1,0:T(8,128)S(1)}, u32[]{:S(2)}, u32[]{:S(2)}) %collective-permute-start.26) | collective-permute-done | bytes 139296 | tf_op jit(solution)/shard_map/ppermute | solution.py:405
  74.4 2.0 %collective-permute-done.27.refs_4_ = f32[272,128]{1,0:T(8,128)S(1)} collective-permute-done((f32[272,128]{1,0:T(8,128)S(1)}, f32[272,128]{1,0:T(8,128)S(1)}, u32[]{:S(2)}, u32[]{:S(2)}) %collective-permute-start.27) | collective-permute-done | bytes 139296 | tf_op jit(solution)/shard_map/ppermute | solution.py:405
  76.4 0.7 collective-permute-done.28.refs_5_
  77.1 1.3 %collective-permute-done.30.refs_7_ = f32[272,128]{1,0:T(8,128)S(1)} collective-permute-done((f32[272,128]{1,0:T(8,128)S(1)}, f32[272,128]{1,0:T(8,128)S(1)}, u32[]{:S(2)}, u32[]{:S(2)}) %collective-permute-start.30) | collective-permute-done | bytes 139296 | tf_op jit(solution)/shard_map/ppermute | solution.py:405
  78.5 12.3 %collective-permute-start.31 = (f32[136,128]{1,0:T(8,128)S(1)}, f32[136,128]{1,0:T(8,128)S(1)}, u32[]{:S(2)}, u32[]{:S(2)}) collective-permute-start(f32[136,128]{1,0:T(8,128)S(1)} %get-tuple-element.64), channel_id=1, source_target_pairs={{0,8},{1,9},{2,10},{3,11},{4,12},{5,13},{6,14},{7,15},{8,0},{9,1},... | collective-permute-start | bytes 208904 | tf_op jit(solution)/shard_map/ppermute | solution.py:405
  90.8 0.9 collective-permute-done.31.other
  91.7 0.8 shard_map.69
  (51 shorter events, 3.3 us)
Async XLA Ops:
  0.0 4.5 %copy-start.3 = (s32[128]{0:T(128)S(1)}, s32[128]{0:T(128)}, u32[]{:S(2)}) copy-start(s32[128]{0:T(128)} %param.6) | copy-start | bytes 1540
  0.0 10.6 %copy-start = (s32[16384]{0:T(1024)S(1)}, s32[16384]{0:T(1024)}, u32[]{:S(2)}) copy-start(s32[16384]{0:T(1024)} %param.7) | copy-start | bytes 196612
  0.0 10.6 %copy-start.1 = (s32[16384]{0:T(1024)S(1)}, s32[16384]{0:T(1024)}, u32[]{:S(2)}) copy-start(s32[16384]{0:T(1024)} %param.8) | copy-start | bytes 196612
  0.0 10.6 %copy-start.2 = (s32[16384]{0:T(1024)S(1)}, s32[16384]{0:T(1024)}, u32[]{:S(2)}) copy-start(s32[16384]{0:T(1024)} %param.9) | copy-start | bytes 196612
  2.4 11.3 %collective-permute-start.16 = (f32[4,128,640]{2,1,0:T(8,128)S(1)}, f32[4,128,640]{2,1,0:T(8,128)S(1)}, u32[]{:S(2)}, u32[]{:S(2)}) collective-permute-start(f32[4,128,640]{2,1,0:T(8,128)S(1)} %get-tuple-element.51), channel_id=1, source_target_pairs={{0,8},{1,9},{2,10},{3,11},{4,12},{5,13},{6,14},{7,15},{8,0},{9,1},... | collective-permute-start | bytes 3932168 | tf_op jit(solution)/shard_map/ppermute | solution.py:405
  3.9 23.3 %collective-permute-start = (f32[4,128,1024]{2,1,0:T(8,128)S(1)}, f32[4,128,1024]{2,1,0:T(8,128)S(1)}, u32[]{:S(2)}, u32[]{:S(2)}) collective-permute-start(f32[4,128,1024]{2,1,0:T(8,128)S(1)} %get-tuple-element.36), channel_id=1, source_target_pairs={{0,8},{1,9},{2,10},{3,11},{4,12},{5,13},{6,14},{7,15},{8,0},{9,1},... | collective-permute-start | bytes 6291464 | tf_op jit(solution)/shard_map/ppermute | solution.py:405
  3.9 7.9 %collective-permute-start.13 = (f32[2,128,384]{2,1,0:T(8,128)S(1)}, f32[2,128,384]{2,1,0:T(8,128)S(1)}, u32[]{:S(2)}, u32[]{:S(2)}) collective-permute-start(f32[2,128,384]{2,1,0:T(8,128)S(1)} %get-tuple-element.49), channel_id=1, source_target_pairs={{0,8},{1,9},{2,10},{3,11},{4,12},{5,13},{6,14},{7,15},{8,0},{9,1},... | collective-permute-start | bytes 1179656 | tf_op jit(solution)/shard_map/ppermute | solution.py:405
  4.4 7.1 %collective-permute-start.1 = (f32[128,256]{1,0:T(8,128)S(1)}, f32[128,256]{1,0:T(8,128)S(1)}, u32[]{:S(2)}, u32[]{:S(2)}) collective-permute-start(f32[128,256]{1,0:T(8,128)S(1)} %get-tuple-element.38), channel_id=1, source_target_pairs={{0,8},{1,9},{2,10},{3,11},{4,12},{5,13},{6,14},{7,15},{8,0},{9,1},... | collective-permute-start | bytes 393224 | tf_op jit(solution)/shard_map/ppermute | solution.py:405
  4.5 5.8 %collective-permute-start.2 = (s32[1,128]{1,0:T(1,128)S(1)}, s32[1,128]{1,0:T(1,128)S(1)}, u32[]{:S(2)}, u32[]{:S(2)}) collective-permute-start(s32[1,128]{1,0:T(1,128)S(1)} %bitcast.34), channel_id=1, source_target_pairs={{0,8},{1,9},{2,10},{3,11},{4,12},{5,13},{6,14},{7,15},{8,0},{9,1},... | collective-permute-start | bytes 1544 | tf_op jit(solution)/shard_map/ppermute | solution.py:405
  10.3 3.4 %collective-permute-start.12 = (f32[2,128,384]{2,1,0:T(8,128)S(1)}, f32[2,128,384]{2,1,0:T(8,128)S(1)}, u32[]{:S(2)}, u32[]{:S(2)}) collective-permute-start(f32[2,128,384]{2,1,0:T(8,128)S(1)} %get-tuple-element.47), channel_id=1, source_target_pairs={{0,8},{1,9},{2,10},{3,11},{4,12},{5,13},{6,14},{7,15},{8,0},{9,1},... | collective-permute-start | bytes 1179656 | tf_op jit(solution)/shard_map/ppermute | solution.py:405
  12.3 11.2 %collective-permute-start.14 = (f32[16,96,128]{2,1,0:T(8,128)S(1)}, f32[16,96,128]{2,1,0:T(8,128)S(1)}, u32[]{:S(2)}, u32[]{:S(2)}) collective-permute-start(f32[16,96,128]{2,1,0:T(8,128)S(1)} %shard_map.64), channel_id=1, source_target_pairs={{0,3},{1,2},{2,1},{3,0},{4,7},{5,6},{6,5},{7,4},{8,9},{9,8},{10,11... | collective-permute-start | bytes 2359304 | tf_op jit(solution)/shard_map/ppermute | solution.py:405
  14.6 12.1 %collective-permute-start.19 = (f32[16,80,128]{2,1,0:T(8,128)S(1)}, f32[16,80,128]{2,1,0:T(8,128)S(1)}, u32[]{:S(2)}, u32[]{:S(2)}) collective-permute-start(f32[16,80,128]{2,1,0:T(8,128)S(1)} %get-tuple-element.55), channel_id=1, source_target_pairs={{0,16},{1,17},{2,18},{3,19},{4,20},{5,21},{6,22},{7,23},{8,56},{9,... | collective-permute-start | bytes 1966088 | tf_op jit(solution)/shard_map/ppermute | solution.py:405
  19.2 12.1 %collective-permute-start.17 = (f32[16,96,128]{2,1,0:T(8,128)S(1)}, f32[16,96,128]{2,1,0:T(8,128)S(1)}, u32[]{:S(2)}, u32[]{:S(2)}) collective-permute-start(f32[16,96,128]{2,1,0:T(8,128)S(1)} %get-tuple-element.53), channel_id=1, source_target_pairs={{0,68},{1,69},{2,70},{3,71},{4,64},{5,65},{6,66},{7,67},{8,12},{9,... | collective-permute-start | bytes 2359304 | tf_op jit(solution)/shard_map/ppermute | solution.py:405
  23.6 11.0 %collective-permute-start.15 = (f32[8,96,128]{2,1,0:T(8,128)S(1)}, f32[8,96,128]{2,1,0:T(8,128)S(1)}, u32[]{:S(2)}, u32[]{:S(2)}) collective-permute-start(f32[8,96,128]{2,1,0:T(8,128)S(1)} %get-tuple-element.68), channel_id=1, source_target_pairs={{0,68},{1,69},{2,70},{3,71},{4,64},{5,65},{6,66},{7,67},{8,12},{9,... | collective-permute-start | bytes 1179656 | tf_op jit(solution)/shard_map/ppermute | solution.py:405
  26.8 9.8 %collective-permute-start.20 = (f32[8,80,128]{2,1,0:T(8,128)S(1)}, f32[8,80,128]{2,1,0:T(8,128)S(1)}, u32[]{:S(2)}, u32[]{:S(2)}) collective-permute-start(f32[8,80,128]{2,1,0:T(8,128)S(1)} %get-tuple-element.74), channel_id=1, source_target_pairs={{0,3},{1,2},{2,1},{3,0},{4,7},{5,6},{6,5},{7,4},{8,9},{9,8},{10,11... | collective-permute-start | bytes 983048 | tf_op jit(solution)/shard_map/ppermute | solution.py:405
  27.8 13.7 %collective-permute-start.3 = (f32[16,96,128]{2,1,0:T(8,128)S(1)}, f32[16,96,128]{2,1,0:T(8,128)S(1)}, u32[]{:S(2)}, u32[]{:S(2)}) collective-permute-start(f32[16,96,128]{2,1,0:T(8,128)S(1)} %shard_map.58), channel_id=1, source_target_pairs={{0,3},{1,2},{2,1},{3,0},{4,7},{5,6},{6,5},{7,4},{8,9},{9,8},{10,11... | collective-permute-start | bytes 2359304 | tf_op jit(solution)/shard_map/ppermute | solution.py:405
  30.2 12.8 %collective-permute-start.5 = (f32[16,96,128]{2,1,0:T(8,128)S(1)}, f32[16,96,128]{2,1,0:T(8,128)S(1)}, u32[]{:S(2)}, u32[]{:S(2)}) collective-permute-start(f32[16,96,128]{2,1,0:T(8,128)S(1)} %get-tuple-element.42), channel_id=1, source_target_pairs={{0,68},{1,69},{2,70},{3,71},{4,64},{5,65},{6,66},{7,67},{8,12},{9,... | collective-permute-start | bytes 2359304 | tf_op jit(solution)/shard_map/ppermute | solution.py:405
  31.4 8.3 %collective-permute-start.18 = (f32[8,96,128]{2,1,0:T(8,128)S(1)}, f32[8,96,128]{2,1,0:T(8,128)S(1)}, u32[]{:S(2)}, u32[]{:S(2)}) collective-permute-start(f32[8,96,128]{2,1,0:T(8,128)S(1)} %get-tuple-element.66), channel_id=1, source_target_pairs={{0,16},{1,17},{2,18},{3,19},{4,20},{5,21},{6,22},{7,23},{8,56},{9,... | collective-permute-start | bytes 1179656 | tf_op jit(solution)/shard_map/ppermute | solution.py:405
  34.6 25.2 %collective-permute-start.21 = (f32[4,96,128]{2,1,0:T(8,128)S(1)}, f32[4,96,128]{2,1,0:T(8,128)S(1)}, u32[]{:S(2)}, u32[]{:S(2)}) collective-permute-start(f32[4,96,128]{2,1,0:T(8,128)S(1)} %get-tuple-element.79), channel_id=1, source_target_pairs={{0,16},{1,17},{2,18},{3,19},{4,20},{5,21},{6,22},{7,23},{8,56},{9,... | collective-permute-start | bytes 589832 | tf_op jit(solution)/shard_map/ppermute | solution.py:405
  36.6 12.2 %collective-permute-start.7 = (f32[16,80,128]{2,1,0:T(8,128)S(1)}, f32[16,80,128]{2,1,0:T(8,128)S(1)}, u32[]{:S(2)}, u32[]{:S(2)}) collective-permute-start(f32[16,80,128]{2,1,0:T(8,128)S(1)} %get-tuple-element.45), channel_id=1, source_target_pairs={{0,16},{1,17},{2,18},{3,19},{4,20},{5,21},{6,22},{7,23},{8,56},{9,... | collective-permute-start | bytes 1966088 | tf_op jit(solution)/shard_map/ppermute | solution.py:405
  39.7 20.7 %collective-permute-start.23 = (f32[4,80,128]{2,1,0:T(8,128)S(1)}, f32[4,80,128]{2,1,0:T(8,128)S(1)}, u32[]{:S(2)}, u32[]{:S(2)}) collective-permute-start(f32[4,80,128]{2,1,0:T(8,128)S(1)} %get-tuple-element.85), channel_id=1, source_target_pairs={{0,68},{1,69},{2,70},{3,71},{4,64},{5,65},{6,66},{7,67},{8,12},{9,... | collective-permute-start | bytes 491528 | tf_op jit(solution)/shard_map/ppermute | solution.py:405
  41.5 18.8 %collective-permute-start.22 = (f32[4,96,128]{2,1,0:T(8,128)S(1)}, f32[4,96,128]{2,1,0:T(8,128)S(1)}, u32[]{:S(2)}, u32[]{:S(2)}) collective-permute-start(f32[4,96,128]{2,1,0:T(8,128)S(1)} %get-tuple-element.77), channel_id=1, source_target_pairs={{0,3},{1,2},{2,1},{3,0},{4,7},{5,6},{6,5},{7,4},{8,9},{9,8},{10,11... | collective-permute-start | bytes 589832 | tf_op jit(solution)/shard_map/ppermute | solution.py:405
  43.0 8.5 %collective-permute-start.4 = (f32[8,96,128]{2,1,0:T(8,128)S(1)}, f32[8,96,128]{2,1,0:T(8,128)S(1)}, u32[]{:S(2)}, u32[]{:S(2)}) collective-permute-start(f32[8,96,128]{2,1,0:T(8,128)S(1)} %get-tuple-element.72), channel_id=1, source_target_pairs={{0,68},{1,69},{2,70},{3,71},{4,64},{5,65},{6,66},{7,67},{8,12},{9,... | collective-permute-start | bytes 1179656 | tf_op jit(solution)/shard_map/ppermute | solution.py:405
  48.8 8.1 %collective-permute-start.6 = (f32[8,96,128]{2,1,0:T(8,128)S(1)}, f32[8,96,128]{2,1,0:T(8,128)S(1)}, u32[]{:S(2)}, u32[]{:S(2)}) collective-permute-start(f32[8,96,128]{2,1,0:T(8,128)S(1)} %get-tuple-element.70), channel_id=1, source_target_pairs={{0,16},{1,17},{2,18},{3,19},{4,20},{5,21},{6,22},{7,23},{8,56},{9,... | collective-permute-start | bytes 1179656 | tf_op jit(solution)/shard_map/ppermute | solution.py:405
  51.6 8.1 %collective-permute-start.8 = (f32[8,80,128]{2,1,0:T(8,128)S(1)}, f32[8,80,128]{2,1,0:T(8,128)S(1)}, u32[]{:S(2)}, u32[]{:S(2)}) collective-permute-start(f32[8,80,128]{2,1,0:T(8,128)S(1)} %get-tuple-element.76), channel_id=1, source_target_pairs={{0,3},{1,2},{2,1},{3,0},{4,7},{5,6},{6,5},{7,4},{8,9},{9,8},{10,11... | collective-permute-start | bytes 983048 | tf_op jit(solution)/shard_map/ppermute | solution.py:405
  56.9 11.3 %collective-permute-start.9 = (f32[4,96,128]{2,1,0:T(8,128)S(1)}, f32[4,96,128]{2,1,0:T(8,128)S(1)}, u32[]{:S(2)}, u32[]{:S(2)}) collective-permute-start(f32[4,96,128]{2,1,0:T(8,128)S(1)} %get-tuple-element.83), channel_id=1, source_target_pairs={{0,16},{1,17},{2,18},{3,19},{4,20},{5,21},{6,22},{7,23},{8,56},{9,... | collective-permute-start | bytes 589832 | tf_op jit(solution)/shard_map/ppermute | solution.py:405
  59.7 9.3 %collective-permute-start.10 = (f32[4,96,128]{2,1,0:T(8,128)S(1)}, f32[4,96,128]{2,1,0:T(8,128)S(1)}, u32[]{:S(2)}, u32[]{:S(2)}) collective-permute-start(f32[4,96,128]{2,1,0:T(8,128)S(1)} %get-tuple-element.81), channel_id=1, source_target_pairs={{0,3},{1,2},{2,1},{3,0},{4,7},{5,6},{6,5},{7,4},{8,9},{9,8},{10,11... | collective-permute-start | bytes 589832 | tf_op jit(solution)/shard_map/ppermute | solution.py:405
  59.8 6.3 %collective-permute-start.11 = (f32[4,80,128]{2,1,0:T(8,128)S(1)}, f32[4,80,128]{2,1,0:T(8,128)S(1)}, u32[]{:S(2)}, u32[]{:S(2)}) collective-permute-start(f32[4,80,128]{2,1,0:T(8,128)S(1)} %get-tuple-element.87), channel_id=1, source_target_pairs={{0,68},{1,69},{2,70},{3,71},{4,64},{5,65},{6,66},{7,67},{8,12},{9,... | collective-permute-start | bytes 491528 | tf_op jit(solution)/shard_map/ppermute | solution.py:405
  60.4 10.7 %collective-permute-start.24 = (f32[272,128]{1,0:T(8,128)S(1)}, f32[272,128]{1,0:T(8,128)S(1)}, u32[]{:S(2)}, u32[]{:S(2)}) collective-permute-start(f32[272,128]{1,0:T(8,128)S(1)} %get-tuple-element.56), channel_id=1, source_target_pairs={{0,53},{1,52},{2,55},{3,54},{4,49},{5,48},{6,51},{7,50},{8,95},{9,... | collective-permute-start | bytes 417800 | tf_op jit(solution)/shard_map/ppermute | solution.py:405
  61.4 11.1 %collective-permute-start.25 = (f32[272,128]{1,0:T(8,128)S(1)}, f32[272,128]{1,0:T(8,128)S(1)}, u32[]{:S(2)}, u32[]{:S(2)}) collective-permute-start(f32[272,128]{1,0:T(8,128)S(1)} %get-tuple-element.57), channel_id=1, source_target_pairs={{0,49},{1,48},{2,51},{3,50},{4,53},{5,52},{6,55},{7,54},{8,27},{9,... | collective-permute-start | bytes 417800 | tf_op jit(solution)/shard_map/ppermute | solution.py:405
  66.1 8.3 %collective-permute-start.26 = (f32[272,128]{1,0:T(8,128)S(1)}, f32[272,128]{1,0:T(8,128)S(1)}, u32[]{:S(2)}, u32[]{:S(2)}) collective-permute-start(f32[272,128]{1,0:T(8,128)S(1)} %get-tuple-element.58), channel_id=1, source_target_pairs={{0,5},{1,4},{2,7},{3,6},{4,1},{5,0},{6,3},{7,2},{8,79},{9,78},{10,... | collective-permute-start | bytes 417800 | tf_op jit(solution)/shard_map/ppermute | solution.py:405
  68.3 8.2 %collective-permute-start.27 = (f32[272,128]{1,0:T(8,128)S(1)}, f32[272,128]{1,0:T(8,128)S(1)}, u32[]{:S(2)}, u32[]{:S(2)}) collective-permute-start(f32[272,128]{1,0:T(8,128)S(1)} %get-tuple-element.59), channel_id=1, source_target_pairs={{0,1},{1,0},{2,3},{3,2},{4,5},{5,4},{6,7},{7,6},{8,11},{9,10},{10,... | collective-permute-start | bytes 417800 | tf_op jit(solution)/shard_map/ppermute | solution.py:405
  69.0 8.1 %collective-permute-start.28 = (f32[272,128]{1,0:T(8,128)S(1)}, f32[272,128]{1,0:T(8,128)S(1)}, u32[]{:S(2)}, u32[]{:S(2)}) collective-permute-start(f32[272,128]{1,0:T(8,128)S(1)} %get-tuple-element.60), channel_id=1, source_target_pairs={{0,52},{1,53},{2,54},{3,55},{4,48},{5,49},{6,50},{7,51},{8,92},{9,... | collective-permute-start | bytes 417800 | tf_op jit(solution)/shard_map/ppermute | solution.py:405
  71.1 6.0 %collective-permute-start.29 = (f32[272,128]{1,0:T(8,128)S(1)}, f32[272,128]{1,0:T(8,128)S(1)}, u32[]{:S(2)}, u32[]{:S(2)}) collective-permute-start(f32[272,128]{1,0:T(8,128)S(1)} %get-tuple-element.61), channel_id=1, source_target_pairs={{0,48},{1,49},{2,50},{3,51},{4,52},{5,53},{6,54},{7,55},{8,24},{9,... | collective-permute-start | bytes 417800 | tf_op jit(solution)/shard_map/ppermute | solution.py:405
  72.5 5.9 %collective-permute-start.30 = (f32[272,128]{1,0:T(8,128)S(1)}, f32[272,128]{1,0:T(8,128)S(1)}, u32[]{:S(2)}, u32[]{:S(2)}) collective-permute-start(f32[272,128]{1,0:T(8,128)S(1)} %get-tuple-element.62), channel_id=1, source_target_pairs={{0,4},{1,5},{2,6},{3,7},{4,0},{5,1},{6,2},{7,3},{8,76},{9,77},{10,... | collective-permute-start | bytes 417800 | tf_op jit(solution)/shard_map/ppermute | solution.py:405
  78.5 13.2 %collective-permute-start.31 = (f32[136,128]{1,0:T(8,128)S(1)}, f32[136,128]{1,0:T(8,128)S(1)}, u32[]{:S(2)}, u32[]{:S(2)}) collective-permute-start(f32[136,128]{1,0:T(8,128)S(1)} %get-tuple-element.64), channel_id=1, source_target_pairs={{0,8},{1,9},{2,10},{3,11},{4,12},{5,13},{6,14},{7,15},{8,0},{9,1},... | collective-permute-start | bytes 208904 | tf_op jit(solution)/shard_map/ppermute | solution.py:405

commit v3 on v2

--- a/solution.py
+++ b/solution.py
@@ -30,7 +30,7 @@
 def flip(index, first, last):
     chip, core = place(index)
     for axis in range(3):
-        kind = core if axis == 2 else 1 - core
+        kind = core if axis == 0 else 1 - core
         mask = first[axis] << kind | last[axis] << (1 - kind)
         chip[axis] = gray(gray(chip[axis]) ^ mask)
     return index_of(chip, core)
@@ -51,7 +51,7 @@
 
 
 def tile_at(core, tile, c, xa, xb):
-    high = jnp.where(core == 1, xb, xa)
+    high = jnp.where(core == 0, xb, xa)
     return tile ^ (c * 4 + high * 2 + (xa ^ xb))
 
 
@@ -196,7 +196,7 @@
     for c in range(2):
         for group in range(8):
             ya, za, zb = group >> 2, group >> 1 & 1, group & 1
-            z_high = jnp.where(core == 0, zb, za)
+            z_high = jnp.where(core == 1, zb, za)
             y_high = jnp.where(core == 1, c ^ ya, ya)
             at = pair ^ (y_high * 4 + z_high * 2 + (za ^ zb))
             start = pl.multiple_of(at * 32, 32)

time: 92.6 us -> 86.4 us (0.933)
  starting transfers between devices: 53 us -> 45.7 us
  waiting for transfers between devices: 27.7 us -> 28.8 us
    ppermute x32, starting transfers between devices: 53 us -> 45.7 us  [permute(): return lax.ppermute(x, AXES, pairs)]
    ppermute x32, waiting for transfers between devices: 27.7 us -> 28.8 us  [permute(): return lax.ppermute(x, AXES, pairs)]
  transfers between devices with their start and end apart: 32 -> 32, of which waited for: 14 -> 14; matrix products, arithmetic and copies ran while one was open for 1% -> 1% of each run, Pallas kernels for 8% -> 9%
where the time goes in v3:
time: 86.4 us; the launch traced here: 86.3 us
  starting transfers between devices  45.7 us (53%)
  waiting for transfers between devices  28.8 us (33%)
  Pallas kernels  10.8 us (12%)
    ppermute x32, starting transfers between devices, permute(): return lax.ppermute(x, AXES, pairs)  45.7 us
    ppermute x32, waiting for transfers between devices, permute(): return lax.ppermute(x, AXES, pairs)  28.8 us
    pallas_call x8, Pallas kernels, gram_call(): call(kernel, [((16, SLOT_ROWS[slot], 128), jnp.float32)] * outs, 'v' * le...  6.26 us
    pallas_call x1, Pallas kernels, cast_call(): call(cast_kernel, [((128, 256), f32), ((2, 128, 384), f32), ((4, 128, 640...  2.38 us
  transfers between devices with their start and end apart: 32, of which 14 were waited for; matrix products, arithmetic and copies ran while one was open for 1% of the time, Pallas kernels for 9%

profile of v3, /device:TPU:1, one launch (start us, length us, event | category | flops | bytes accessed | tf_op | source)
XLA Modules:
  0.0 86.3 jit_solution(713968380331246256)
XLA Ops:
  0.0 2.4 %shard_map.55 = (f32[128,256]{1,0:T(8,128)S(1)}, f32[2,128,384]{2,1,0:T(8,128)S(1)}, f32[4,128,640]{2,1,0:T(8,128)S(1)}, f32[2,128,384]{2,1,0:T(8,128)S(1)}, f32...) custom-call(bf16[128,16384]{1,0:T(8,128)(2,1)} %feat.1), custom_call_target="tpu_custom_call" | custom-call | flops 1000000 | bytes 6291456 | tf_op jit(solution)/shard_map/pallas_call | solution.py:115
  2.4 1.4 %collective-permute-start.16 = (f32[4,128,640]{2,1,0:T(8,128)S(1)}, f32[4,128,640]{2,1,0:T(8,128)S(1)}, u32[]{:S(2)}, u32[]{:S(2)}) collective-permute-start(f32[4,128,640]{2,1,0:T(8,128)S(1)} %get-tuple-element.51), channel_id=1, source_target_pairs={{0,8},{1,9},{2,10},{3,11},{4,12},{5,13},{6,14},{7,15},{8,0},{9,1},... | collective-permute-start | bytes 3932168 | tf_op jit(solution)/shard_map/ppermute | solution.py:405
  3.9 0.4 collective-permute-start.13
  4.5 0.4 collective-permute-start.2
  4.9 5.4 %collective-permute-done.2.other_salt = s32[1,128]{1,0:T(1,128)S(1)} collective-permute-done((s32[1,128]{1,0:T(1,128)S(1)}, s32[1,128]{1,0:T(1,128)S(1)}, u32[]{:S(2)}, u32[]{:S(2)}) %collective-permute-start.2) | collective-permute-done | bytes 544 | tf_op jit(solution)/shard_map/ppermute | solution.py:405
  10.3 0.4 collective-permute-start.12
  10.6 0.9 shard_map.63
  11.5 0.3 shard_map.56
  11.8 0.4 shard_map.64
  12.3 2.7 %collective-permute-start.14 = (f32[16,96,128]{2,1,0:T(8,128)S(1)}, f32[16,96,128]{2,1,0:T(8,128)S(1)}, u32[]{:S(2)}, u32[]{:S(2)}) collective-permute-start(f32[16,96,128]{2,1,0:T(8,128)S(1)} %shard_map.64), channel_id=1, source_target_pairs={{0,1},{1,0},{2,3},{3,2},{4,5},{5,4},{6,7},{7,6},{8,11},{9,10},{10,... | collective-permute-start | bytes 2359304 | tf_op jit(solution)/shard_map/ppermute | solution.py:405
  15.0 0.9 %shard_map.66 = (f32[16,80,128]{2,1,0:T(8,128)S(1)}, f32[16,80,128]{2,1,0:T(8,128)S(1)}) custom-call(bf16[4,128,640]{2,1,0:T(8,128)(2,1)S(1)} %get-tuple-element.50.own, f32[4,128,640]{2,1,0:T(8,128)S(1)} %collective-permute-done.16.other, bf16[2,256,256]{2,1,0:T(8,128)(2,1)S(1)} %get-tuple-element.39.q, s32[256,128]{1,0:T(8,128)S(1)} %get-tuple-element.40.salt, ...), custom_call_target="tpu_custom_call" | custom-call | flops 128000000 | bytes 3145728 | tf_op jit(solution)/shard_map/pallas_call | solution.py:332
  15.9 1.7 %collective-permute-start.19 = (f32[16,80,128]{2,1,0:T(8,128)S(1)}, f32[16,80,128]{2,1,0:T(8,128)S(1)}, u32[]{:S(2)}, u32[]{:S(2)}) collective-permute-start(f32[16,80,128]{2,1,0:T(8,128)S(1)} %get-tuple-element.55), channel_id=1, source_target_pairs={{0,48},{1,49},{2,50},{3,51},{4,52},{5,53},{6,54},{7,55},{8,24},{9,... | collective-permute-start | bytes 1966088 | tf_op jit(solution)/shard_map/ppermute | solution.py:405
  17.6 0.7 shard_map.65
  18.3 1.4 %collective-permute-start.17 = (f32[16,96,128]{2,1,0:T(8,128)S(1)}, f32[16,96,128]{2,1,0:T(8,128)S(1)}, u32[]{:S(2)}, u32[]{:S(2)}) collective-permute-start(f32[16,96,128]{2,1,0:T(8,128)S(1)} %get-tuple-element.53), channel_id=1, source_target_pairs={{0,68},{1,69},{2,70},{3,71},{4,64},{5,65},{6,66},{7,67},{8,12},{9,... | collective-permute-start | bytes 2359304 | tf_op jit(solution)/shard_map/ppermute | solution.py:405
  19.7 0.6 shard_map.62
  20.3 4.4 %collective-permute-done.14 = f32[16,96,128]{2,1,0:T(8,128)S(1)} collective-permute-done((f32[16,96,128]{2,1,0:T(8,128)S(1)}, f32[16,96,128]{2,1,0:T(8,128)S(1)}, u32[]{:S(2)}, u32[]{:S(2)}) %collective-permute-start.14) | collective-permute-done | bytes 786464 | tf_op jit(solution)/shard_map/ppermute | solution.py:405
  24.8 1.5 %collective-permute-start.15 = (f32[8,96,128]{2,1,0:T(8,128)S(1)}, f32[8,96,128]{2,1,0:T(8,128)S(1)}, u32[]{:S(2)}, u32[]{:S(2)}) collective-permute-start(f32[8,96,128]{2,1,0:T(8,128)S(1)} %get-tuple-element.68), channel_id=1, source_target_pairs={{0,68},{1,69},{2,70},{3,71},{4,64},{5,65},{6,66},{7,67},{8,12},{9,... | collective-permute-start | bytes 1179656 | tf_op jit(solution)/shard_map/ppermute | solution.py:405
  26.4 2.6 %collective-permute-start.20 = (f32[8,80,128]{2,1,0:T(8,128)S(1)}, f32[8,80,128]{2,1,0:T(8,128)S(1)}, u32[]{:S(2)}, u32[]{:S(2)}) collective-permute-start(f32[8,80,128]{2,1,0:T(8,128)S(1)} %get-tuple-element.74), channel_id=1, source_target_pairs={{0,1},{1,0},{2,3},{3,2},{4,5},{5,4},{6,7},{7,6},{8,11},{9,10},{10,... | collective-permute-start | bytes 983048 | tf_op jit(solution)/shard_map/ppermute | solution.py:405
  29.0 0.6 shard_map.58
  29.6 0.3 collective-permute-start.3
  29.9 1.1 %shard_map.59 = (f32[16,96,128]{2,1,0:T(8,128)S(1)}, f32[16,96,128]{2,1,0:T(8,128)S(1)}) custom-call(bf16[8,128,1024]{2,1,0:T(8,128)(2,1)S(1)} %get-tuple-element.35.mine, f32[4,128,1024]{2,1,0:T(8,128)S(1)} %collective-permute-done.other, bf16[2,256,256]{2,1,0:T(8,128)(2,1)S(1)} %get-tuple-element.39.q, s32[256,128]{1,0:T(8,128)S(1)} %get-tuple-element.40.salt, ...), custom_call_target="tpu_custom_call" | custom-call | flops 192000000 | bytes 3145728 | tf_op jit(solution)/shard_map/pallas_call | solution.py:332
  31.0 0.9 %collective-permute-start.5 = (f32[16,96,128]{2,1,0:T(8,128)S(1)}, f32[16,96,128]{2,1,0:T(8,128)S(1)}, u32[]{:S(2)}, u32[]{:S(2)}) collective-permute-start(f32[16,96,128]{2,1,0:T(8,128)S(1)} %get-tuple-element.42), channel_id=1, source_target_pairs={{0,68},{1,69},{2,70},{3,71},{4,64},{5,65},{6,66},{7,67},{8,12},{9,... | collective-permute-start | bytes 2359304 | tf_op jit(solution)/shard_map/ppermute | solution.py:405
  32.0 1.5 %collective-permute-start.18 = (f32[8,96,128]{2,1,0:T(8,128)S(1)}, f32[8,96,128]{2,1,0:T(8,128)S(1)}, u32[]{:S(2)}, u32[]{:S(2)}) collective-permute-start(f32[8,96,128]{2,1,0:T(8,128)S(1)} %get-tuple-element.66), channel_id=1, source_target_pairs={{0,48},{1,49},{2,50},{3,51},{4,52},{5,53},{6,54},{7,55},{8,24},{9,... | collective-permute-start | bytes 1179656 | tf_op jit(solution)/shard_map/ppermute | solution.py:405
  33.9 0.6 shard_map.57
  34.5 1.2 %shard_map.60 = (f32[16,80,128]{2,1,0:T(8,128)S(1)}, f32[16,80,128]{2,1,0:T(8,128)S(1)}) custom-call(bf16[8,128,1024]{2,1,0:T(8,128)(2,1)S(1)} %get-tuple-element.35.mine, f32[4,128,1024]{2,1,0:T(8,128)S(1)} %collective-permute-done.other, bf16[2,256,256]{2,1,0:T(8,128)(2,1)S(1)} %get-tuple-element.39.q, s32[256,128]{1,0:T(8,128)S(1)} %get-tuple-element.40.salt, ...), custom_call_target="tpu_custom_call" | custom-call | flops 128000000 | bytes 3145728 | tf_op jit(solution)/shard_map/pallas_call | solution.py:332
  35.7 1.5 %collective-permute-start.7 = (f32[16,80,128]{2,1,0:T(8,128)S(1)}, f32[16,80,128]{2,1,0:T(8,128)S(1)}, u32[]{:S(2)}, u32[]{:S(2)}) collective-permute-start(f32[16,80,128]{2,1,0:T(8,128)S(1)} %get-tuple-element.45), channel_id=1, source_target_pairs={{0,48},{1,49},{2,50},{3,51},{4,52},{5,53},{6,54},{7,55},{8,24},{9,... | collective-permute-start | bytes 1966088 | tf_op jit(solution)/shard_map/ppermute | solution.py:405
  37.3 1.7 %collective-permute-done.18 = f32[8,96,128]{2,1,0:T(8,128)S(1)} collective-permute-done((f32[8,96,128]{2,1,0:T(8,128)S(1)}, f32[8,96,128]{2,1,0:T(8,128)S(1)}, u32[]{:S(2)}, u32[]{:S(2)}) %collective-permute-start.18) | collective-permute-done | bytes 393248 | tf_op jit(solution)/shard_map/ppermute | solution.py:405
  39.0 0.6 collective-permute-start.23
  39.7 2.6 %collective-permute-done.3 = f32[16,96,128]{2,1,0:T(8,128)S(1)} collective-permute-done((f32[16,96,128]{2,1,0:T(8,128)S(1)}, f32[16,96,128]{2,1,0:T(8,128)S(1)}, u32[]{:S(2)}, u32[]{:S(2)}) %collective-permute-start.3) | collective-permute-done | bytes 786464 | tf_op jit(solution)/shard_map/ppermute | solution.py:405
  42.3 2.5 %collective-permute-start.22 = (f32[4,96,128]{2,1,0:T(8,128)S(1)}, f32[4,96,128]{2,1,0:T(8,128)S(1)}, u32[]{:S(2)}, u32[]{:S(2)}) collective-permute-start(f32[4,96,128]{2,1,0:T(8,128)S(1)} %get-tuple-element.77), channel_id=1, source_target_pairs={{0,1},{1,0},{2,3},{3,2},{4,5},{5,4},{6,7},{7,6},{8,11},{9,10},{10,... | collective-permute-start | bytes 589832 | tf_op jit(solution)/shard_map/ppermute | solution.py:405
  45.3 2.9 %collective-permute-done.7 = f32[16,80,128]{2,1,0:T(8,128)S(1)} collective-permute-done((f32[16,80,128]{2,1,0:T(8,128)S(1)}, f32[16,80,128]{2,1,0:T(8,128)S(1)}, u32[]{:S(2)}, u32[]{:S(2)}) %collective-permute-start.7) | collective-permute-done | bytes 655392 | tf_op jit(solution)/shard_map/ppermute | solution.py:405
  48.2 1.5 %collective-permute-start.6 = (f32[8,96,128]{2,1,0:T(8,128)S(1)}, f32[8,96,128]{2,1,0:T(8,128)S(1)}, u32[]{:S(2)}, u32[]{:S(2)}) collective-permute-start(f32[8,96,128]{2,1,0:T(8,128)S(1)} %get-tuple-element.70), channel_id=1, source_target_pairs={{0,48},{1,49},{2,50},{3,51},{4,52},{5,53},{6,54},{7,55},{8,24},{9,... | collective-permute-start | bytes 1179656 | tf_op jit(solution)/shard_map/ppermute | solution.py:405
  49.7 2.2 %collective-permute-done.4 = f32[8,96,128]{2,1,0:T(8,128)S(1)} collective-permute-done((f32[8,96,128]{2,1,0:T(8,128)S(1)}, f32[8,96,128]{2,1,0:T(8,128)S(1)}, u32[]{:S(2)}, u32[]{:S(2)}) %collective-permute-start.4) | collective-permute-done | bytes 393248 | tf_op jit(solution)/shard_map/ppermute | solution.py:405
  52.2 2.9 %collective-permute-done.6 = f32[8,96,128]{2,1,0:T(8,128)S(1)} collective-permute-done((f32[8,96,128]{2,1,0:T(8,128)S(1)}, f32[8,96,128]{2,1,0:T(8,128)S(1)}, u32[]{:S(2)}, u32[]{:S(2)}) %collective-permute-start.6) | collective-permute-done | bytes 393248 | tf_op jit(solution)/shard_map/ppermute | solution.py:405
  55.1 1.5 %collective-permute-start.9 = (f32[4,96,128]{2,1,0:T(8,128)S(1)}, f32[4,96,128]{2,1,0:T(8,128)S(1)}, u32[]{:S(2)}, u32[]{:S(2)}) collective-permute-start(f32[4,96,128]{2,1,0:T(8,128)S(1)} %get-tuple-element.83), channel_id=1, source_target_pairs={{0,48},{1,49},{2,50},{3,51},{4,52},{5,53},{6,54},{7,55},{8,24},{9,... | collective-permute-start | bytes 589832 | tf_op jit(solution)/shard_map/ppermute | solution.py:405
  56.6 2.8 %collective-permute-done.8 = f32[8,80,128]{2,1,0:T(8,128)S(1)} collective-permute-done((f32[8,80,128]{2,1,0:T(8,128)S(1)}, f32[8,80,128]{2,1,0:T(8,128)S(1)}, u32[]{:S(2)}, u32[]{:S(2)}) %collective-permute-start.8) | collective-permute-done | bytes 327712 | tf_op jit(solution)/shard_map/ppermute | solution.py:405
  59.6 0.9 %collective-permute-start.11 = (f32[4,80,128]{2,1,0:T(8,128)S(1)}, f32[4,80,128]{2,1,0:T(8,128)S(1)}, u32[]{:S(2)}, u32[]{:S(2)}) collective-permute-start(f32[4,80,128]{2,1,0:T(8,128)S(1)} %get-tuple-element.87), channel_id=1, source_target_pairs={{0,68},{1,69},{2,70},{3,71},{4,64},{5,65},{6,66},{7,67},{8,12},{9,... | collective-permute-start | bytes 491528 | tf_op jit(solution)/shard_map/ppermute | solution.py:405
  60.6 1.5 %collective-permute-start.24 = (f32[272,128]{1,0:T(8,128)S(1)}, f32[272,128]{1,0:T(8,128)S(1)}, u32[]{:S(2)}, u32[]{:S(2)}) collective-permute-start(f32[272,128]{1,0:T(8,128)S(1)} %get-tuple-element.56), channel_id=1, source_target_pairs={{0,23},{1,22},{2,21},{3,20},{4,19},{5,18},{6,17},{7,16},{8,125},{9... | collective-permute-start | bytes 417800 | tf_op jit(solution)/shard_map/ppermute | solution.py:405
  62.1 4.0 %collective-permute-start.25 = (f32[272,128]{1,0:T(8,128)S(1)}, f32[272,128]{1,0:T(8,128)S(1)}, u32[]{:S(2)}, u32[]{:S(2)}) collective-permute-start(f32[272,128]{1,0:T(8,128)S(1)} %get-tuple-element.57), channel_id=1, source_target_pairs={{0,19},{1,18},{2,17},{3,16},{4,23},{5,22},{6,21},{7,20},{8,57},{9,... | collective-permute-start | bytes 417800 | tf_op jit(solution)/shard_map/ppermute | solution.py:405
  66.0 1.5 %collective-permute-start.26 = (f32[272,128]{1,0:T(8,128)S(1)}, f32[272,128]{1,0:T(8,128)S(1)}, u32[]{:S(2)}, u32[]{:S(2)}) collective-permute-start(f32[272,128]{1,0:T(8,128)S(1)} %get-tuple-element.58), channel_id=1, source_target_pairs={{0,7},{1,6},{2,5},{3,4},{4,3},{5,2},{6,1},{7,0},{8,77},{9,76},{10,... | collective-permute-start | bytes 417800 | tf_op jit(solution)/shard_map/ppermute | solution.py:405
  67.6 0.3 collective-permute-start.27
  67.9 5.6 %collective-permute-start.28 = (f32[272,128]{1,0:T(8,128)S(1)}, f32[272,128]{1,0:T(8,128)S(1)}, u32[]{:S(2)}, u32[]{:S(2)}) collective-permute-start(f32[272,128]{1,0:T(8,128)S(1)} %get-tuple-element.60), channel_id=1, source_target_pairs={{0,20},{1,21},{2,22},{3,23},{4,16},{5,17},{6,18},{7,19},{8,124},{9... | collective-permute-start | bytes 417800 | tf_op jit(solution)/shard_map/ppermute | solution.py:405
  73.5 2.7 %collective-permute-start.30 = (f32[272,128]{1,0:T(8,128)S(1)}, f32[272,128]{1,0:T(8,128)S(1)}, u32[]{:S(2)}, u32[]{:S(2)}) collective-permute-start(f32[272,128]{1,0:T(8,128)S(1)} %get-tuple-element.62), channel_id=1, source_target_pairs={{0,4},{1,5},{2,6},{3,7},{4,0},{5,1},{6,2},{7,3},{8,76},{9,77},{10,... | collective-permute-start | bytes 417800 | tf_op jit(solution)/shard_map/ppermute | solution.py:405
  76.4 0.6 collective-permute-done.28.refs_5_
  77.0 1.9 %collective-permute-done.29.refs_6_ = f32[272,128]{1,0:T(8,128)S(1)} collective-permute-done((f32[272,128]{1,0:T(8,128)S(1)}, f32[272,128]{1,0:T(8,128)S(1)}, u32[]{:S(2)}, u32[]{:S(2)}) %collective-permute-start.29) | collective-permute-done | bytes 139296 | tf_op jit(solution)/shard_map/ppermute | solution.py:405
  79.1 5.5 %collective-permute-start.31 = (f32[136,128]{1,0:T(8,128)S(1)}, f32[136,128]{1,0:T(8,128)S(1)}, u32[]{:S(2)}, u32[]{:S(2)}) collective-permute-start(f32[136,128]{1,0:T(8,128)S(1)} %get-tuple-element.64), channel_id=1, source_target_pairs={{0,8},{1,9},{2,10},{3,11},{4,12},{5,13},{6,14},{7,15},{8,0},{9,1},... | collective-permute-start | bytes 208904 | tf_op jit(solution)/shard_map/ppermute | solution.py:405
  84.6 0.9 %collective-permute-done.31.other = f32[136,128]{1,0:T(8,128)S(1)} collective-permute-done((f32[136,128]{1,0:T(8,128)S(1)}, f32[136,128]{1,0:T(8,128)S(1)}, u32[]{:S(2)}, u32[]{:S(2)}) %collective-permute-start.31) | collective-permute-done | bytes 69664 | tf_op jit(solution)/shard_map/ppermute | solution.py:405
  85.5 0.8 shard_map.69
  (51 shorter events, 2.4 us)
Async XLA Ops:
  0.0 4.5 %copy-start.3 = (s32[128]{0:T(128)S(1)}, s32[128]{0:T(128)}, u32[]{:S(2)}) copy-start(s32[128]{0:T(128)} %param.6) | copy-start | bytes 1540
  0.0 10.6 %copy-start = (s32[16384]{0:T(1024)S(1)}, s32[16384]{0:T(1024)}, u32[]{:S(2)}) copy-start(s32[16384]{0:T(1024)} %param.7) | copy-start | bytes 196612
  0.0 10.6 %copy-start.1 = (s32[16384]{0:T(1024)S(1)}, s32[16384]{0:T(1024)}, u32[]{:S(2)}) copy-start(s32[16384]{0:T(1024)} %param.8) | copy-start | bytes 196612
  0.0 10.6 %copy-start.2 = (s32[16384]{0:T(1024)S(1)}, s32[16384]{0:T(1024)}, u32[]{:S(2)}) copy-start(s32[16384]{0:T(1024)} %param.9) | copy-start | bytes 196612
  2.4 12.6 %collective-permute-start.16 = (f32[4,128,640]{2,1,0:T(8,128)S(1)}, f32[4,128,640]{2,1,0:T(8,128)S(1)}, u32[]{:S(2)}, u32[]{:S(2)}) collective-permute-start(f32[4,128,640]{2,1,0:T(8,128)S(1)} %get-tuple-element.51), channel_id=1, source_target_pairs={{0,8},{1,9},{2,10},{3,11},{4,12},{5,13},{6,14},{7,15},{8,0},{9,1},... | collective-permute-start | bytes 3932168 | tf_op jit(solution)/shard_map/ppermute | solution.py:405
  3.9 25.1 %collective-permute-start = (f32[4,128,1024]{2,1,0:T(8,128)S(1)}, f32[4,128,1024]{2,1,0:T(8,128)S(1)}, u32[]{:S(2)}, u32[]{:S(2)}) collective-permute-start(f32[4,128,1024]{2,1,0:T(8,128)S(1)} %get-tuple-element.36), channel_id=1, source_target_pairs={{0,8},{1,9},{2,10},{3,11},{4,12},{5,13},{6,14},{7,15},{8,0},{9,1},... | collective-permute-start | bytes 6291464 | tf_op jit(solution)/shard_map/ppermute | solution.py:405
  3.9 7.9 %collective-permute-start.13 = (f32[2,128,384]{2,1,0:T(8,128)S(1)}, f32[2,128,384]{2,1,0:T(8,128)S(1)}, u32[]{:S(2)}, u32[]{:S(2)}) collective-permute-start(f32[2,128,384]{2,1,0:T(8,128)S(1)} %get-tuple-element.49), channel_id=1, source_target_pairs={{0,8},{1,9},{2,10},{3,11},{4,12},{5,13},{6,14},{7,15},{8,0},{9,1},... | collective-permute-start | bytes 1179656 | tf_op jit(solution)/shard_map/ppermute | solution.py:405
  4.4 7.1 %collective-permute-start.1 = (f32[128,256]{1,0:T(8,128)S(1)}, f32[128,256]{1,0:T(8,128)S(1)}, u32[]{:S(2)}, u32[]{:S(2)}) collective-permute-start(f32[128,256]{1,0:T(8,128)S(1)} %get-tuple-element.38), channel_id=1, source_target_pairs={{0,8},{1,9},{2,10},{3,11},{4,12},{5,13},{6,14},{7,15},{8,0},{9,1},... | collective-permute-start | bytes 393224 | tf_op jit(solution)/shard_map/ppermute | solution.py:405
  4.5 5.8 %collective-permute-start.2 = (s32[1,128]{1,0:T(1,128)S(1)}, s32[1,128]{1,0:T(1,128)S(1)}, u32[]{:S(2)}, u32[]{:S(2)}) collective-permute-start(s32[1,128]{1,0:T(1,128)S(1)} %bitcast.34), channel_id=1, source_target_pairs={{0,8},{1,9},{2,10},{3,11},{4,12},{5,13},{6,14},{7,15},{8,0},{9,1},... | collective-permute-start | bytes 1544 | tf_op jit(solution)/shard_map/ppermute | solution.py:405
  10.3 4.7 %collective-permute-start.12 = (f32[2,128,384]{2,1,0:T(8,128)S(1)}, f32[2,128,384]{2,1,0:T(8,128)S(1)}, u32[]{:S(2)}, u32[]{:S(2)}) collective-permute-start(f32[2,128,384]{2,1,0:T(8,128)S(1)} %get-tuple-element.47), channel_id=1, source_target_pairs={{0,8},{1,9},{2,10},{3,11},{4,12},{5,13},{6,14},{7,15},{8,0},{9,1},... | collective-permute-start | bytes 1179656 | tf_op jit(solution)/shard_map/ppermute | solution.py:405
  12.3 12.4 %collective-permute-start.14 = (f32[16,96,128]{2,1,0:T(8,128)S(1)}, f32[16,96,128]{2,1,0:T(8,128)S(1)}, u32[]{:S(2)}, u32[]{:S(2)}) collective-permute-start(f32[16,96,128]{2,1,0:T(8,128)S(1)} %shard_map.64), channel_id=1, source_target_pairs={{0,1},{1,0},{2,3},{3,2},{4,5},{5,4},{6,7},{7,6},{8,11},{9,10},{10,... | collective-permute-start | bytes 2359304 | tf_op jit(solution)/shard_map/ppermute | solution.py:405
  15.9 10.4 %collective-permute-start.19 = (f32[16,80,128]{2,1,0:T(8,128)S(1)}, f32[16,80,128]{2,1,0:T(8,128)S(1)}, u32[]{:S(2)}, u32[]{:S(2)}) collective-permute-start(f32[16,80,128]{2,1,0:T(8,128)S(1)} %get-tuple-element.55), channel_id=1, source_target_pairs={{0,48},{1,49},{2,50},{3,51},{4,52},{5,53},{6,54},{7,55},{8,24},{9,... | collective-permute-start | bytes 1966088 | tf_op jit(solution)/shard_map/ppermute | solution.py:405
  18.3 13.6 %collective-permute-start.17 = (f32[16,96,128]{2,1,0:T(8,128)S(1)}, f32[16,96,128]{2,1,0:T(8,128)S(1)}, u32[]{:S(2)}, u32[]{:S(2)}) collective-permute-start(f32[16,96,128]{2,1,0:T(8,128)S(1)} %get-tuple-element.53), channel_id=1, source_target_pairs={{0,68},{1,69},{2,70},{3,71},{4,64},{5,65},{6,66},{7,67},{8,12},{9,... | collective-permute-start | bytes 2359304 | tf_op jit(solution)/shard_map/ppermute | solution.py:405
  24.8 8.9 %collective-permute-start.15 = (f32[8,96,128]{2,1,0:T(8,128)S(1)}, f32[8,96,128]{2,1,0:T(8,128)S(1)}, u32[]{:S(2)}, u32[]{:S(2)}) collective-permute-start(f32[8,96,128]{2,1,0:T(8,128)S(1)} %get-tuple-element.68), channel_id=1, source_target_pairs={{0,68},{1,69},{2,70},{3,71},{4,64},{5,65},{6,66},{7,67},{8,12},{9,... | collective-permute-start | bytes 1179656 | tf_op jit(solution)/shard_map/ppermute | solution.py:405
  26.4 9.3 %collective-permute-start.20 = (f32[8,80,128]{2,1,0:T(8,128)S(1)}, f32[8,80,128]{2,1,0:T(8,128)S(1)}, u32[]{:S(2)}, u32[]{:S(2)}) collective-permute-start(f32[8,80,128]{2,1,0:T(8,128)S(1)} %get-tuple-element.74), channel_id=1, source_target_pairs={{0,1},{1,0},{2,3},{3,2},{4,5},{5,4},{6,7},{7,6},{8,11},{9,10},{10,... | collective-permute-start | bytes 983048 | tf_op jit(solution)/shard_map/ppermute | solution.py:405
  29.6 12.7 %collective-permute-start.3 = (f32[16,96,128]{2,1,0:T(8,128)S(1)}, f32[16,96,128]{2,1,0:T(8,128)S(1)}, u32[]{:S(2)}, u32[]{:S(2)}) collective-permute-start(f32[16,96,128]{2,1,0:T(8,128)S(1)} %shard_map.58), channel_id=1, source_target_pairs={{0,1},{1,0},{2,3},{3,2},{4,5},{5,4},{6,7},{7,6},{8,11},{9,10},{10,... | collective-permute-start | bytes 2359304 | tf_op jit(solution)/shard_map/ppermute | solution.py:405
  31.0 13.9 %collective-permute-start.5 = (f32[16,96,128]{2,1,0:T(8,128)S(1)}, f32[16,96,128]{2,1,0:T(8,128)S(1)}, u32[]{:S(2)}, u32[]{:S(2)}) collective-permute-start(f32[16,96,128]{2,1,0:T(8,128)S(1)} %get-tuple-element.42), channel_id=1, source_target_pairs={{0,68},{1,69},{2,70},{3,71},{4,64},{5,65},{6,66},{7,67},{8,12},{9,... | collective-permute-start | bytes 2359304 | tf_op jit(solution)/shard_map/ppermute | solution.py:405
  32.0 7.0 %collective-permute-start.18 = (f32[8,96,128]{2,1,0:T(8,128)S(1)}, f32[8,96,128]{2,1,0:T(8,128)S(1)}, u32[]{:S(2)}, u32[]{:S(2)}) collective-permute-start(f32[8,96,128]{2,1,0:T(8,128)S(1)} %get-tuple-element.66), channel_id=1, source_target_pairs={{0,48},{1,49},{2,50},{3,51},{4,52},{5,53},{6,54},{7,55},{8,24},{9,... | collective-permute-start | bytes 1179656 | tf_op jit(solution)/shard_map/ppermute | solution.py:405
  33.8 25.8 %collective-permute-start.21 = (f32[4,96,128]{2,1,0:T(8,128)S(1)}, f32[4,96,128]{2,1,0:T(8,128)S(1)}, u32[]{:S(2)}, u32[]{:S(2)}) collective-permute-start(f32[4,96,128]{2,1,0:T(8,128)S(1)} %get-tuple-element.79), channel_id=1, source_target_pairs={{0,48},{1,49},{2,50},{3,51},{4,52},{5,53},{6,54},{7,55},{8,24},{9,... | collective-permute-start | bytes 589832 | tf_op jit(solution)/shard_map/ppermute | solution.py:405
  35.7 12.4 %collective-permute-start.7 = (f32[16,80,128]{2,1,0:T(8,128)S(1)}, f32[16,80,128]{2,1,0:T(8,128)S(1)}, u32[]{:S(2)}, u32[]{:S(2)}) collective-permute-start(f32[16,80,128]{2,1,0:T(8,128)S(1)} %get-tuple-element.45), channel_id=1, source_target_pairs={{0,48},{1,49},{2,50},{3,51},{4,52},{5,53},{6,54},{7,55},{8,24},{9,... | collective-permute-start | bytes 1966088 | tf_op jit(solution)/shard_map/ppermute | solution.py:405
  39.0 21.5 %collective-permute-start.23 = (f32[4,80,128]{2,1,0:T(8,128)S(1)}, f32[4,80,128]{2,1,0:T(8,128)S(1)}, u32[]{:S(2)}, u32[]{:S(2)}) collective-permute-start(f32[4,80,128]{2,1,0:T(8,128)S(1)} %get-tuple-element.85), channel_id=1, source_target_pairs={{0,68},{1,69},{2,70},{3,71},{4,64},{5,65},{6,66},{7,67},{8,12},{9,... | collective-permute-start | bytes 491528 | tf_op jit(solution)/shard_map/ppermute | solution.py:405
  42.3 18.2 %collective-permute-start.22 = (f32[4,96,128]{2,1,0:T(8,128)S(1)}, f32[4,96,128]{2,1,0:T(8,128)S(1)}, u32[]{:S(2)}, u32[]{:S(2)}) collective-permute-start(f32[4,96,128]{2,1,0:T(8,128)S(1)} %get-tuple-element.77), channel_id=1, source_target_pairs={{0,1},{1,0},{2,3},{3,2},{4,5},{5,4},{6,7},{7,6},{8,11},{9,10},{10,... | collective-permute-start | bytes 589832 | tf_op jit(solution)/shard_map/ppermute | solution.py:405
  44.9 7.0 %collective-permute-start.4 = (f32[8,96,128]{2,1,0:T(8,128)S(1)}, f32[8,96,128]{2,1,0:T(8,128)S(1)}, u32[]{:S(2)}, u32[]{:S(2)}) collective-permute-start(f32[8,96,128]{2,1,0:T(8,128)S(1)} %get-tuple-element.72), channel_id=1, source_target_pairs={{0,68},{1,69},{2,70},{3,71},{4,64},{5,65},{6,66},{7,67},{8,12},{9,... | collective-permute-start | bytes 1179656 | tf_op jit(solution)/shard_map/ppermute | solution.py:405
  48.2 6.9 %collective-permute-start.6 = (f32[8,96,128]{2,1,0:T(8,128)S(1)}, f32[8,96,128]{2,1,0:T(8,128)S(1)}, u32[]{:S(2)}, u32[]{:S(2)}) collective-permute-start(f32[8,96,128]{2,1,0:T(8,128)S(1)} %get-tuple-element.70), channel_id=1, source_target_pairs={{0,48},{1,49},{2,50},{3,51},{4,52},{5,53},{6,54},{7,55},{8,24},{9,... | collective-permute-start | bytes 1179656 | tf_op jit(solution)/shard_map/ppermute | solution.py:405
  51.9 7.4 %collective-permute-start.8 = (f32[8,80,128]{2,1,0:T(8,128)S(1)}, f32[8,80,128]{2,1,0:T(8,128)S(1)}, u32[]{:S(2)}, u32[]{:S(2)}) collective-permute-start(f32[8,80,128]{2,1,0:T(8,128)S(1)} %get-tuple-element.76), channel_id=1, source_target_pairs={{0,1},{1,0},{2,3},{3,2},{4,5},{5,4},{6,7},{7,6},{8,11},{9,10},{10,... | collective-permute-start | bytes 983048 | tf_op jit(solution)/shard_map/ppermute | solution.py:405
  55.1 12.5 %collective-permute-start.9 = (f32[4,96,128]{2,1,0:T(8,128)S(1)}, f32[4,96,128]{2,1,0:T(8,128)S(1)}, u32[]{:S(2)}, u32[]{:S(2)}) collective-permute-start(f32[4,96,128]{2,1,0:T(8,128)S(1)} %get-tuple-element.83), channel_id=1, source_target_pairs={{0,48},{1,49},{2,50},{3,51},{4,52},{5,53},{6,54},{7,55},{8,24},{9,... | collective-permute-start | bytes 589832 | tf_op jit(solution)/shard_map/ppermute | solution.py:405
  59.4 8.5 %collective-permute-start.10 = (f32[4,96,128]{2,1,0:T(8,128)S(1)}, f32[4,96,128]{2,1,0:T(8,128)S(1)}, u32[]{:S(2)}, u32[]{:S(2)}) collective-permute-start(f32[4,96,128]{2,1,0:T(8,128)S(1)} %get-tuple-element.81), channel_id=1, source_target_pairs={{0,1},{1,0},{2,3},{3,2},{4,5},{5,4},{6,7},{7,6},{8,11},{9,10},{10,... | collective-permute-start | bytes 589832 | tf_op jit(solution)/shard_map/ppermute | solution.py:405
  59.6 6.4 %collective-permute-start.11 = (f32[4,80,128]{2,1,0:T(8,128)S(1)}, f32[4,80,128]{2,1,0:T(8,128)S(1)}, u32[]{:S(2)}, u32[]{:S(2)}) collective-permute-start(f32[4,80,128]{2,1,0:T(8,128)S(1)} %get-tuple-element.87), channel_id=1, source_target_pairs={{0,68},{1,69},{2,70},{3,71},{4,64},{5,65},{6,66},{7,67},{8,12},{9,... | collective-permute-start | bytes 491528 | tf_op jit(solution)/shard_map/ppermute | solution.py:405
  60.6 12.9 %collective-permute-start.24 = (f32[272,128]{1,0:T(8,128)S(1)}, f32[272,128]{1,0:T(8,128)S(1)}, u32[]{:S(2)}, u32[]{:S(2)}) collective-permute-start(f32[272,128]{1,0:T(8,128)S(1)} %get-tuple-element.56), channel_id=1, source_target_pairs={{0,23},{1,22},{2,21},{3,20},{4,19},{5,18},{6,17},{7,16},{8,125},{9... | collective-permute-start | bytes 417800 | tf_op jit(solution)/shard_map/ppermute | solution.py:405
  62.1 11.5 %collective-permute-start.25 = (f32[272,128]{1,0:T(8,128)S(1)}, f32[272,128]{1,0:T(8,128)S(1)}, u32[]{:S(2)}, u32[]{:S(2)}) collective-permute-start(f32[272,128]{1,0:T(8,128)S(1)} %get-tuple-element.57), channel_id=1, source_target_pairs={{0,19},{1,18},{2,17},{3,16},{4,23},{5,22},{6,21},{7,20},{8,57},{9,... | collective-permute-start | bytes 417800 | tf_op jit(solution)/shard_map/ppermute | solution.py:405
  66.0 10.2 %collective-permute-start.26 = (f32[272,128]{1,0:T(8,128)S(1)}, f32[272,128]{1,0:T(8,128)S(1)}, u32[]{:S(2)}, u32[]{:S(2)}) collective-permute-start(f32[272,128]{1,0:T(8,128)S(1)} %get-tuple-element.58), channel_id=1, source_target_pairs={{0,7},{1,6},{2,5},{3,4},{4,3},{5,2},{6,1},{7,0},{8,77},{9,76},{10,... | collective-permute-start | bytes 417800 | tf_op jit(solution)/shard_map/ppermute | solution.py:405
  67.6 8.9 %collective-permute-start.27 = (f32[272,128]{1,0:T(8,128)S(1)}, f32[272,128]{1,0:T(8,128)S(1)}, u32[]{:S(2)}, u32[]{:S(2)}) collective-permute-start(f32[272,128]{1,0:T(8,128)S(1)} %get-tuple-element.59), channel_id=1, source_target_pairs={{0,3},{1,2},{2,1},{3,0},{4,7},{5,6},{6,5},{7,4},{8,9},{9,8},{10,11... | collective-permute-start | bytes 417800 | tf_op jit(solution)/shard_map/ppermute | solution.py:405
  67.9 9.1 %collective-permute-start.28 = (f32[272,128]{1,0:T(8,128)S(1)}, f32[272,128]{1,0:T(8,128)S(1)}, u32[]{:S(2)}, u32[]{:S(2)}) collective-permute-start(f32[272,128]{1,0:T(8,128)S(1)} %get-tuple-element.60), channel_id=1, source_target_pairs={{0,20},{1,21},{2,22},{3,23},{4,16},{5,17},{6,18},{7,19},{8,124},{9... | collective-permute-start | bytes 417800 | tf_op jit(solution)/shard_map/ppermute | solution.py:405
  73.5 5.4 %collective-permute-start.29 = (f32[272,128]{1,0:T(8,128)S(1)}, f32[272,128]{1,0:T(8,128)S(1)}, u32[]{:S(2)}, u32[]{:S(2)}) collective-permute-start(f32[272,128]{1,0:T(8,128)S(1)} %get-tuple-element.61), channel_id=1, source_target_pairs={{0,16},{1,17},{2,18},{3,19},{4,20},{5,21},{6,22},{7,23},{8,56},{9,... | collective-permute-start | bytes 417800 | tf_op jit(solution)/shard_map/ppermute | solution.py:405
  73.5 5.5 %collective-permute-start.30 = (f32[272,128]{1,0:T(8,128)S(1)}, f32[272,128]{1,0:T(8,128)S(1)}, u32[]{:S(2)}, u32[]{:S(2)}) collective-permute-start(f32[272,128]{1,0:T(8,128)S(1)} %get-tuple-element.62), channel_id=1, source_target_pairs={{0,4},{1,5},{2,6},{3,7},{4,0},{5,1},{6,2},{7,3},{8,76},{9,77},{10,... | collective-permute-start | bytes 417800 | tf_op jit(solution)/shard_map/ppermute | solution.py:405
  79.1 6.4 %collective-permute-start.31 = (f32[136,128]{1,0:T(8,128)S(1)}, f32[136,128]{1,0:T(8,128)S(1)}, u32[]{:S(2)}, u32[]{:S(2)}) collective-permute-start(f32[136,128]{1,0:T(8,128)S(1)} %get-tuple-element.64), channel_id=1, source_target_pairs={{0,8},{1,9},{2,10},{3,11},{4,12},{5,13},{6,14},{7,15},{8,0},{9,1},... | collective-permute-start | bytes 208904 | tf_op jit(solution)/shard_map/ppermute | solution.py:405
